TPU v7x, 32 devices: a whole 2x2x4 slice. The times are simulated.
32 devices in a mesh: dp: 16 (over z, y, x), rep: 2 (over core).
Axes of the slice: x: 2, y: 2, z: 4, core: 2. Of those that a mesh axis runs over, the one named last changes fastest.
Arguments:
- pooled: bfloat16 [16, 128, 8192], P(None, ('dp', 'rep')), may hold values from -6 to 6
- slot_of_block: int32 [128], replicated, may hold values from 0 to 127, each once
- dense_part: bfloat16 [128, 8192], P(None, ('dp', 'rep')), may hold values from -6 to 6
- labels: int32 [8192], P(('dp', 'rep')), may hold values 0 or 1
- sample_weight: float32 [8192], P(('dp', 'rep')), may hold values from 0.5 to 18, as said below
- proj_wide: bfloat16 [6, 256, 128], replicated, may hold values from -0.375 to 0.375
- proj_mid: bfloat16 [4, 64, 128], replicated, may hold values from -0.75 to 0.75
- proj_narrow: bfloat16 [16, 16, 128], replicated, may hold values from -1.5 to 1.5
- cross_in: bfloat16 [2, 3456, 256], replicated, may hold values from -0.109375 to 0.109375
- cross_out: bfloat16 [2, 256, 3456], replicated, may hold values from -0.375 to 0.375
- cross_bias: float32 [2, 3456], replicated, may hold values from -3 to 3
- head_weight: float32 [3456], replicated, may hold values from -0.24 to 0.24
Outputs:
- pooled_grad: float32 [16, 128, 8192], P(None, ('dp', 'rep'))
- grad_cross_in: float32 [2, 3456, 256], P(None, ('dp', 'rep'))
- grad_cross_out: float32 [2, 256, 3456], P(None, None, ('dp', 'rep'))
- grad_bias: float32 [2, 3456], P(None, ('dp', 'rep'))
Inputs may be any that keep to these rules, and one draw needn't show every extreme that they name: `slot_of_block`: each number of 0 to 127 appears once. `sample_weight`: positive.
All inputs are finite; a program needn't handle non-finite values. No bound on the sum of `labels` on one device may be relied on, other than what follows from the above.
Results may differ from a plain program's by a relative error of at most 0.014.
Values may be sent and summed in bfloat16 or wider, within the bound.
No kernel may reach another device: no remote copies, remote signals or barrier semaphores. Data moves between devices by JAX's collectives and lax.ppermute only.
A program may use at most 128 MiB of HBM per device.

v0:
```python
import jax
import jax.numpy as jnp
from jax import lax
from jax.sharding import PartitionSpec as P

BLOCK_WIDTH = 16
WIDE_TABLES = 6
MID_TABLES = 4
NARROW_TABLES = 16
WIDE_WIDTH = 256
MID_WIDTH = 64
NARROW_WIDTH = 16
PROJECTED = 128
LAYERS = 2
BLOCKS = 128


def table_layout():
    first_end = WIDE_TABLES * (WIDE_WIDTH // BLOCK_WIDTH)
    second_end = first_end + MID_TABLES * (MID_WIDTH // BLOCK_WIDTH)
    return (
        (0, first_end, WIDE_TABLES, WIDE_WIDTH),
        (first_end, second_end, MID_TABLES, MID_WIDTH),
        (second_end, BLOCKS, NARROW_TABLES, NARROW_WIDTH),
    )


def project_tables(logical, proj_tables):
    row_count = logical.shape[2]
    outputs = []
    for layout, proj_table in zip(table_layout(), proj_tables):
        block_start, block_end, table_count, table_width = layout
        pieces = logical[:, block_start:block_end].reshape(
            BLOCK_WIDTH, table_count, table_width // BLOCK_WIDTH, row_count
        )
        matrix = proj_table.reshape(table_count, table_width // BLOCK_WIDTH, BLOCK_WIDTH, PROJECTED)
        result = jnp.einsum("tkco,ctkr->tor", matrix, pieces, preferred_element_type=jnp.float32)
        outputs.append(result.reshape(table_count * PROJECTED, row_count))
    return jnp.concatenate(outputs, 0)


def project_back(proj_grad, proj_tables):
    row_count = proj_grad.shape[1]
    outputs = []
    offset = 0
    for layout, proj_table in zip(table_layout(), proj_tables):
        block_start, block_end, table_count, table_width = layout
        piece = proj_grad[offset : offset + table_count * PROJECTED].reshape(
            table_count, PROJECTED, row_count
        )
        offset = offset + table_count * PROJECTED
        matrix = proj_table.reshape(table_count, table_width // BLOCK_WIDTH, BLOCK_WIDTH, PROJECTED)
        result = jnp.einsum("tkco,tor->ctkr", matrix, piece, preferred_element_type=jnp.float32)
        outputs.append(result.reshape(BLOCK_WIDTH, block_end - block_start, row_count))
    return jnp.concatenate(outputs, 1)


def block_step(
    slots,
    dense_part,
    labels,
    sample_weight,
    slot_of_block,
    proj_tables,
    cross_in,
    cross_out,
    cross_bias,
    head_weight,
):
    logical = jnp.take(slots, slot_of_block, axis=1)
    projected = project_tables(logical, proj_tables)
    start = jnp.concatenate([dense_part.astype(jnp.float32), projected], 0).astype(jnp.bfloat16)
    start_full = start.astype(jnp.float32)
    layer_inputs = [start]
    hidden_list = []
    gate_list = []
    current = start
    for layer in range(LAYERS):
        hidden = jnp.einsum(
            "wk,wr->kr", cross_in[layer], current, preferred_element_type=jnp.float32
        ).astype(jnp.bfloat16)
        gate = (
            jnp.einsum("kw,kr->wr", cross_out[layer], hidden, preferred_element_type=jnp.float32)
            + cross_bias[layer][:, None]
        )
        current = (start_full * gate + current.astype(jnp.float32)).astype(jnp.bfloat16)
        hidden_list.append(hidden)
        gate_list.append(gate)
        layer_inputs.append(current)
    logit = jnp.dot(head_weight, current.astype(jnp.float32), precision=lax.Precision.HIGHEST)
    signal = sample_weight * (jax.nn.sigmoid(logit) - labels.astype(jnp.float32))
    upstream = head_weight[:, None] * signal[None, :]
    start_grad = jnp.zeros(start_full.shape, jnp.float32)
    in_terms = [None] * LAYERS
    out_terms = [None] * LAYERS
    bias_terms = [None] * LAYERS
    for layer in reversed(range(LAYERS)):
        gate_grad = start_full * upstream
        bias_terms[layer] = jnp.sum(gate_grad, axis=1)
        gate_low = gate_grad.astype(jnp.bfloat16)
        out_terms[layer] = jnp.einsum(
            "wr,kr->wk", gate_low, hidden_list[layer], preferred_element_type=jnp.float32
        )
        hidden_grad = jnp.einsum(
            "kw,wr->kr", cross_out[layer], gate_low, preferred_element_type=jnp.float32
        ).astype(jnp.bfloat16)
        in_terms[layer] = jnp.einsum(
            "wr,kr->wk", layer_inputs[layer], hidden_grad, preferred_element_type=jnp.float32
        )
        start_grad = start_grad + gate_list[layer] * upstream
        upstream = upstream + jnp.einsum(
            "wk,kr->wr", cross_in[layer], hidden_grad, preferred_element_type=jnp.float32
        )
    start_grad = start_grad + upstream
    proj_grad = start_grad[PROJECTED:].astype(jnp.bfloat16)
    logical_grad = project_back(proj_grad, proj_tables)
    slot_grad = jnp.zeros(logical_grad.shape, jnp.float32).at[:, slot_of_block, :].set(logical_grad)
    return (slot_grad, jnp.stack(in_terms), jnp.stack(out_terms), jnp.stack(bias_terms))


def body(
    pooled,
    slot_of_block,
    dense_part,
    labels,
    sample_weight,
    proj_wide,
    proj_mid,
    proj_narrow,
    cross_in,
    cross_out,
    cross_bias,
    head_weight,
):
    dp_count = lax.axis_size("dp")
    rep_count = lax.axis_size("rep")
    devices = dp_count * rep_count
    row_count = labels.shape[0]
    blocks_here = pooled.shape[1]
    batch_rows = row_count * devices
    layer_count = cross_in.shape[0]
    received = lax.all_to_all(
        pooled[:, None], ("dp", "rep"), split_axis=3, concat_axis=1, tiled=True
    )
    slots = received.reshape(BLOCK_WIDTH, BLOCKS, row_count)
    local_total = jnp.sum(sample_weight)
    proj_tables = (proj_wide, proj_mid, proj_narrow)
    slot_grad, in_term, out_term, bias_term = block_step(
        slots,
        dense_part,
        labels,
        sample_weight,
        slot_of_block,
        proj_tables,
        cross_in,
        cross_out,
        cross_bias,
        head_weight,
    )
    returned = lax.all_to_all(
        slot_grad.reshape(BLOCK_WIDTH, devices, blocks_here, row_count),
        ("dp", "rep"),
        split_axis=1,
        concat_axis=3,
        tiled=True,
    )
    returned = returned.reshape(BLOCK_WIDTH, blocks_here, batch_rows)
    weight_terms = jnp.concatenate([in_term, out_term], 0)
    total_row = jnp.full((1, bias_term.shape[1]), local_total, jnp.float32)
    bias_terms = jnp.concatenate([bias_term, total_row], 0)
    weight_sums = lax.psum_scatter(weight_terms, ("dp", "rep"), scatter_dimension=1, tiled=True)
    bias_sums = lax.psum_scatter(bias_terms, ("dp", "rep"), scatter_dimension=1, tiled=True)
    total = bias_sums[layer_count, 0]
    scale = batch_rows / total
    grad_in = weight_sums[:layer_count] * scale
    grad_out = jnp.swapaxes(weight_sums[layer_count:], 1, 2) * scale
    grad_bias = bias_sums[:layer_count] * scale
    return (returned * scale, grad_in, grad_out, grad_bias)


def solution(mesh):
    return jax.shard_map(
        body,
        mesh=mesh,
        in_specs=(
            P(None, ("dp", "rep"), None),
            P(),
            P(None, ("dp", "rep")),
            P(("dp", "rep")),
            P(("dp", "rep")),
            P(),
            P(),
            P(),
            P(),
            P(),
            P(),
            P(),
        ),
        out_specs=(
            P(None, ("dp", "rep"), None),
            P(None, ("dp", "rep"), None),
            P(None, None, ("dp", "rep")),
            P(None, ("dp", "rep")),
        ),
        check_vma=False,
    )
```

profile of v0, /device:TPU:0, one launch (start us, length us, event | category | flops | bytes accessed | tf_op | source)
XLA Modules:
  0.0 435.4 jit_solution(6802570207956939293)
XLA Ops:
  7.2 11.3 %copy.68 = bf16[16,4,8192]{0,1,2:T(4,128)(2,1)} copy(bf16[16,4,8192]{2,1,0:T(4,128)(2,1)} %param.12) | data formatting | bytes 2097152 | tf_op args[0]
  18.5 8.1 %bitcast_bitcast_fusion = bf16[8192,1,4,16]{3,2,1,0:T(4,128)(2,1)} fusion(bf16[16,4,8192]{0,1,2:T(4,128)(2,1)} %copy.68), kind=kLoop, calls=%fused_computation.81 | loop fusion | bytes 2097152
  26.6 11.3 %reshape.130 = bf16[32,2,8192]{2,1,0:T(2,128)(2,1)} reshape(bf16[8192,1,4,16]{3,2,1,0:T(4,128)(2,1)} %bitcast_bitcast_fusion) | data formatting | bytes 2097152
  37.9 7.3 %all-to-all-start = ((bf16[32,2,8192]{2,1,0:T(2,128)(2,1)}), bf16[32,2,8192]{2,1,0:T(2,128)(2,1)S(1)}, u32[]{:S(2)}, u32[]{:S(2)}) async-start(bf16[32,2,8192]{2,1,0:T(2,128)(2,1)} %reshape.130), calls=%async_computation | async-start | bytes 2097152 | tf_op jit(solution)/shard_map/all_to_all | solution.py:142
  47.3 24.1 %all-to-all-done = bf16[32,2,8192]{2,1,0:T(2,128)(2,1)S(1)} async-done(((bf16[32,2,8192]{2,1,0:T(2,128)(2,1)}), bf16[32,2,8192]{2,1,0:T(2,128)(2,1)S(1)}, u32[]{:S(2)}, u32[]{:S(2)}) %all-to-all-start) | async-done | bytes 1048608 | tf_op jit(solution)/shard_map/all_to_all | solution.py:142
  71.4 7.5 %reshape.131 = bf16[8192,1,4,16]{3,2,1,0:T(4,128)(2,1)} reshape(bf16[32,2,8192]{2,1,0:T(2,128)(2,1)S(1)} %all-to-all-done) | data formatting | bytes 2097152
  79.0 8.6 %copy.85 = bf16[16,1,4,32,256]{4,3,0,2,1:T(8,128)(2,1)S(1)} copy(bf16[16,1,4,32,256]{0,2,4,3,1:T(4,128)(2,1)} %bitcast.154) | data formatting | bytes 2097152 | tf_op jit(solution)/shard_map/all_to_all | solution.py:142
  89.5 1.3 convolution_convert_fusion
  92.4 2.3 fusion.37
  94.9 2.6 fusion.8
  99.0 1.7 fusion.13
  103.7 1.8 fusion.11
  106.3 0.9 copy-done.1
  108.7 1.6 pad_maximum_fusion
  110.3 24.9 %copy.81 = f32[4,3456,256]{2,0,1:T(4,128)} copy(f32[4,3456,256]{2,1,0:T(8,128)S(1)} %pad_maximum_fusion) | data formatting | bytes 28311552 | tf_op jit(solution)/shard_map/concatenate | solution.py:168
  135.2 5.6 %fusion.4 = bf16[3456,256]{0,1:T(8,128)(2,1)S(1)} fusion(f32[3456,256]{0,1:T(8,128)} %copy-done.1, bf16[256,256]{1,0:T(8,128)(2,1)S(1)} %fusion.40, f32[3456,256]{0,1:T(8,128)} %copy-done.2, f32[3456,256]{0,1:T(8,128)} %get-tuple-element.25, f32[256]{0:T(256)S(1)} %get-tuple-element.23, f32[3456]{0:T(1024)S(1)} %copy-done.11, bf16[2,3456,256]{2,1,0:T(8,128)(2,1)} %param.20), kind=kOutput, calls=%fused_computation.22 | convolution fusion | flops 459177984 | bytes 14301696 | tf_op jit(solution)/shard_map/wk,kr->wr/dot_general | solution.py:111
  142.9 1.6 broadcast_in_dim.24
  144.5 15.8 %scatter_fusion = f32[16,128,256]{2,0,1:T(8,128)} fusion(f32[16,128,256]{2,0,1:T(8,128)} %broadcast_in_dim.24, s32[128]{0:T(128)S(1)} %copy-done.17, f32[128,16,256]{2,1,0:T(8,128)S(1)} %maximum_bitcast_fusion), kind=kCustom, calls=%fused_computation.1 | custom fusion | bytes 6291968 | tf_op jit(solution)/shard_map/scatter | solution.py:117
  160.4 3.6 all-to-all-start.1
  164.8 91.5 %all-reduce = f32[3,3456]{1,0:T(4,128)S(1)} all-reduce(f32[3,3456]{1,0:T(4,128)S(1)} %maximum_maximum_fusion), channel_id=2, replica_groups=mesh['dp'=16,'rep'=2] {'dp','rep'}, use_global_device_ids=true, to_apply=%region_4.5.clone | all-reduce | flops 10368 | bytes 82944
  258.3 1.2 copy.80
  259.6 2.0 mul.82
  261.6 164.8 %all-reduce.4.cloned.1.call-done = f32[4,3456,256]{2,0,1:T(4,128)} async-done(((f32[4,3456,256]{2,0,1:T(4,128)}), f32[4,3456,256]{2,0,1:T(4,128)}) %all-reduce.4.cloned.1.call-update) | async-done | bytes 14155792
  426.4 2.1 fusion.52
  (88 shorter events, 16.7 us)
Async XLA Ops:
  7.2 84.6 %copy-start = (bf16[6,256,128]{2,1,0:T(8,128)(2,1)S(1)}, bf16[6,256,128]{2,1,0:T(8,128)(2,1)}, u32[]{:S(2)}) copy-start(bf16[6,256,128]{2,1,0:T(8,128)(2,1)} %param.17) | copy-start | bytes 1179652
  26.6 18.7 %copy-start.10 = (f32[3456]{0:T(1024)S(1)}, f32[3456]{0:T(1024)}, u32[]{:S(2)}) copy-start(f32[3456]{0:T(1024)} %param.23) | copy-start | bytes 41476
  26.6 19.3 %copy-start.9 = (bf16[128,256]{1,0:T(8,128)(2,1)S(1)}, bf16[128,256]{1,0:T(8,128)(2,1)}, u32[]{:S(2)}) copy-start(bf16[128,256]{1,0:T(8,128)(2,1)} %param.14) | copy-start | bytes 196612
  26.6 20.0 %copy-start.20 = (s32[128]{0:T(128)S(1)}, s32[128]{0:T(128)}, u32[]{:S(2)}) copy-start(s32[128]{0:T(128)} %param.13) | copy-start | bytes 1540
  26.6 20.0 %copy-start.12 = (f32[2,3456]{1,0:T(2,128)S(1)}, f32[2,3456]{1,0:T(2,128)}, u32[]{:S(2)}) copy-start(f32[2,3456]{1,0:T(2,128)} %param.22) | copy-start | bytes 82948
  37.9 33.5 %all-to-all-start = ((bf16[32,2,8192]{2,1,0:T(2,128)(2,1)}), bf16[32,2,8192]{2,1,0:T(2,128)(2,1)S(1)}, u32[]{:S(2)}, u32[]{:S(2)}) async-start(bf16[32,2,8192]{2,1,0:T(2,128)(2,1)} %reshape.130), calls=%async_computation | async-start | bytes 2097152 | tf_op jit(solution)/shard_map/all_to_all | solution.py:142
  45.2 381.2 %all-reduce.4.cloned.1.call-start = ((), (), s32[]{:S(2)}) async-start(), calls=%async_computation.2 | async-start | bytes 28311552
  46.6 32.3 %copy-start.16 = (s32[128]{0:T(128)}, s32[128]{0:T(128)S(1)}, u32[]{:S(2)}) copy-start(s32[128]{0:T(128)S(1)} %compare_select_fusion) | copy-start | bytes 1540
  88.2 1.0 copy-start.6
  91.5 0.8 copy-start.5
  92.4 2.5 copy-start.3
  92.4 2.5 copy-start.14
  94.9 2.7 copy-start.4
  98.3 0.7 copy-start.15
  99.0 1.8 copy-start.2
  99.0 1.8 copy-start.18
  99.0 1.8 copy-start.19
  99.0 2.4 copy-start.11
  105.4 1.8 copy-start.1
  140.9 1.1 copy-start.7
  140.9 1.2 copy-start.8
  142.8 1.8 copy-start.17
  160.4 3.6 copy-start.13
  160.4 97.7 %all-to-all-start.1 = ((f32[16,32,4,256]{3,0,2,1:T(8,128)}), f32[16,32,4,256]{3,0,2,1:T(8,128)S(1)}, u32[]{:S(2)}, u32[]{:S(2)}) async-start(f32[16,32,4,256]{3,0,2,1:T(8,128)} %bitcast.42), calls=%async_computation.1 | async-start | bytes 4194304 | tf_op jit(solution)/shard_map/all_to_all | solution.py:160
Sparse Core Ops, SparseCore 0:
  135.4 291.0 all-reduce.3
where the time goes:
time: 437 us; the launch traced here: 435 us
  waiting for transfers between devices  189 us (43%)
  local copies, waits for them, and re-layouts  101 us (23%)
  blocking collectives  91.5 us (21%)
  matrix products  22.5 us (5%)
  between operations  15.2 us (3%)
  starting transfers between devices  10.9 us (2%)
  other arithmetic  5.55 us (1%)
    unnamed x2, waiting for transfers between devices  165 us
    unnamed x1, blocking collectives  91.5 us
    unnamed x49, local copies, waits for them, and re-layouts  41.3 us
    concatenate x1, local copies, waits for them, and re-layouts, body(): weight_terms = jnp.concatenate([in_term, out_term], 0)  24.9 us
    all_to_all x1, waiting for transfers between devices, body(): lax.all_to_all(pooled[:, None], ('dp', 'rep'), split_axis=3, concat_axis=...  24.1 us
    scatter x1, local copies, waits for them, and re-layouts, block_step(): jnp.zeros(logical_grad.shape, jnp.float32).at[:, slot_of_block, :]  15.8 us
    all_to_all x2, local copies, waits for them, and re-layouts, body(): lax.all_to_all(pooled[:, None], ('dp', 'rep'), split_axis=3, concat_axis=...  9.17 us
  transfers between devices with their start and end apart: 3, of which 2 were waited for; matrix products, arithmetic and copies ran while one was open for 7% of the time, Pallas kernels for 0%

commit v1 on v0

v1 whole, which is shorter than its diff:
```python
import jax
import jax.numpy as jnp
from jax import lax
from jax.experimental import pallas as pl
from jax.experimental.pallas import tpu as pltpu
from jax.sharding import PartitionSpec as P

BLOCK_WIDTH = 16
PROJECTED = 128
LANES = 128
AXES = ("dp", "rep")
NN = (((1,), (0,)), ((), ()))
NT = (((1,), (1,)), ((), ()))
BF = jnp.bfloat16
F32 = jnp.float32


def dot(a, b, dims=NN):
    return lax.dot_general(a, b, dims, preferred_element_type=F32)


def exchange_basis(dp_count, rep_count):
    bits = dp_count.bit_length() - 1
    low = bits - 2
    masks = []
    if low <= 2:
        masks += [1 << i for i in range(max(low, 0))]
    else:
        for base in range(0, low, 2):
            masks += [1 << base, 3 << base]
    if bits >= 2:
        masks += [1 << low, 2 << low]
    elif bits == 1:
        masks += [1]
    core = [1 << i for i in range(rep_count.bit_length() - 1)]
    return core, [m * rep_count for m in masks]


def basis_digits(index, masks):
    digits = {}
    for mask in sorted(masks, reverse=True):
        top = mask.bit_length() - 1
        bit = (index >> top) & 1
        digits[mask] = bit
        index = index ^ (bit * mask)
    return digits


def position_of(index, order):
    digits = basis_digits(index, order)
    place = 0
    for mask in order:
        place = place * 2 + digits[mask]
    return place


def pack_kernel(weight_ref, x_ref, out_ref, tmp_ref):
    group, depth, lanes = out_ref.shape
    width, blocks, span = x_ref.shape
    per = span // (group * lanes)
    for c in range(width):
        for m in range(group * per):
            tmp_ref[m, pl.ds(c, blocks, stride=width), :] = x_ref[c, :, m * lanes : (m + 1) * lanes].astype(F32)
    total = jnp.sum(jnp.sum(weight_ref[...], 0, keepdims=True), 1, keepdims=True)
    first = total.astype(BF).astype(F32)
    second = (total - first).astype(BF).astype(F32)
    third = total - first - second
    row = lax.broadcasted_iota(jnp.int32, (8, lanes), 0)
    tail = jnp.where(row == 0, first, jnp.where(row == 1, second, jnp.where(row == 2, third, 0.0)))
    for g in range(group):
        for j in range(blocks):
            for h in range(per):
                out_ref[g, (j * per + h) * width : (j * per + h + 1) * width, :] = tmp_ref[
                    g * per + h, j * width : (j + 1) * width, :
                ].astype(BF)
        out_ref[g, depth - 8 : depth, :] = tail.astype(BF)


def pack(pooled, weight, devices):
    width, blocks, batch = pooled.shape
    rows = batch // devices
    per = rows // LANES
    group = 4
    depth = blocks * per * width + 8
    return pl.pallas_call(
        pack_kernel,
        grid=(devices // group,),
        in_specs=[
            pl.BlockSpec((per, LANES), lambda i: (0, 0)),
            pl.BlockSpec((width, blocks, group * rows), lambda i: (0, 0, i)),
        ],
        out_specs=pl.BlockSpec((group, depth, LANES), lambda i: (i, 0, 0)),
        out_shape=jax.ShapeDtypeStruct((devices, depth, LANES), BF),
        scratch_shapes=[pltpu.VMEM((group * per, blocks * width, LANES), F32)],
        name="pack",
    )(weight.reshape(per, LANES), pooled)


def unpack_kernel(x_ref, out_ref, tmp_ref):
    group, _, rows = x_ref.shape
    width, blocks, _ = out_ref.shape
    lanes = tmp_ref.shape[2]
    per = rows // lanes
    for m in range(group * per):
        at = (m % per) * lanes
        tmp_ref[m] = x_ref[m // per, :, at : at + lanes].astype(F32)
        for c in range(width):
            out_ref[c, :, m * lanes : (m + 1) * lanes] = tmp_ref[m, pl.ds(c, blocks, stride=width), :]


def unpack(received):
    width = BLOCK_WIDTH
    devices, both, rows = received.shape
    blocks = both // width
    group = 4
    return pl.pallas_call(
        unpack_kernel,
        grid=(devices // group,),
        in_specs=[pl.BlockSpec((group, both, rows), lambda i: (i, 0, 0))],
        out_specs=pl.BlockSpec((width, blocks, group * rows), lambda i: (0, 0, i)),
        out_shape=jax.ShapeDtypeStruct((width, blocks, devices * rows), F32),
        scratch_shapes=[pltpu.VMEM((group * rows // LANES, both, LANES), F32)],
        name="unpack",
    )(received)


def make_step(tables, devices, blocks_here):
    def kernel(
        slot_ref,
        x_ref,
        dense_ref,
        row_ref,
        col_ref,
        pt0,
        pt1,
        pt2,
        p0,
        p1,
        p2,
        cit_hbm,
        ci_hbm,
        cot_hbm,
        co_hbm,
        back_ref,
        start,
        layer1,
        low1,
        low0,
        small,
        cit_ref,
        ci_ref,
        cot_ref,
        co_ref,
        low,
        gate0,
        gate1,
        sems,
    ):
        pts, ps = (pt0, pt1, pt2), (p0, p1, p2)
        width, rows = start.shape
        tile_rows = 3 * PROJECTED
        tiles = width // tile_rows
        per = rows // LANES

        names = {"cit": (cit_hbm, cit_ref), "cot": (cot_hbm, cot_ref), "co": (co_hbm, co_ref), "ci": (ci_hbm, ci_ref)}
        uses = [("cit", 0), ("cot", 0), ("cit", 1), ("cot", 1), ("co", 1), ("ci", 1), ("co", 0), ("ci", 0)]

        def fetch(n):
            name, layer = uses[n]
            source, target = names[name]
            return pltpu.make_async_copy(source.at[layer], target.at[layer], sems.at[n])

        for n in range(len(uses)):
            fetch(n).start()

        def tile(i):
            return pl.ds(pl.multiple_of(i * tile_rows, tile_rows), tile_rows)

        def loop(body, init=None):
            if init is None:
                lax.fori_loop(0, tiles, lambda i, c: (body(i), c)[1], 0)
                return None
            return lax.fori_loop(0, tiles, body, init)

        start[0:PROJECTED, :] = dense_ref[...]
        for t, (first, count, kind, index) in enumerate(tables):
            parts = []
            for k in range(count):
                slot = slot_ref[first + k]
                at = (slot % blocks_here) * (per * BLOCK_WIDTH)
                pieces = [
                    x_ref[slot // blocks_here, pl.ds(pl.multiple_of(at + h * BLOCK_WIDTH, 16), BLOCK_WIDTH), :]
                    for h in range(per)
                ]
                parts.append(jnp.concatenate(pieces, 1))
            block = parts[0] if count == 1 else jnp.concatenate(parts, 0)
            start[(t + 1) * PROJECTED : (t + 2) * PROJECTED, :] = dot(pts[kind][index], block).astype(BF)

        fetch(0).wait()
        hidden0 = dot(cit_ref[0], start[...]).astype(BF)
        small[0] = hidden0
        fetch(1).wait()

        def fwd0(i):
            s = start[tile(i), :].astype(F32)
            g = dot(cot_ref[0, tile(i), :], hidden0) + col_ref[tile(i), 0:1]
            gate0[tile(i), :] = g
            layer1[tile(i), :] = (s * g + s).astype(BF)

        loop(fwd0)
        fetch(2).wait()
        hidden1 = dot(cit_ref[1], layer1[...]).astype(BF)
        small[1] = hidden1
        fetch(3).wait()

        def fwd1(i, logit):
            s = start[tile(i), :].astype(F32)
            g = dot(cot_ref[1, tile(i), :], hidden1) + col_ref[tile(i), 1:2]
            gate1[tile(i), :] = g
            last = (s * g + layer1[tile(i), :].astype(F32)).astype(BF).astype(F32)
            term = last * col_ref[tile(i), 2:3]
            return logit + jnp.sum(term.reshape(tile_rows // 8, 8, rows), 0)

        partial = loop(fwd1, jnp.zeros((8, rows), F32))
        logit = jnp.sum(partial, 0, keepdims=True)
        depth = x_ref.shape[1]

        def gather_total(d, carry):
            return carry + x_ref[d][depth - 8 : depth, :].astype(F32)

        terms = lax.fori_loop(0, devices, gather_total, jnp.zeros((8, LANES), F32))
        total = jnp.sum(terms, 0, keepdims=True)[:, 0:1]
        scale = float(rows * devices) / total
        signal = scale * row_ref[0:1, :] * (jax.nn.sigmoid(logit) - row_ref[1:2, :])

        def bwd1(i):
            s = start[tile(i), :].astype(F32)
            low1[tile(i), :] = (s * (col_ref[tile(i), 2:3] * signal)).astype(BF)

        loop(bwd1)
        fetch(4).wait()
        hgrad1 = dot(co_ref[1], low1[...]).astype(BF)
        small[2] = hgrad1
        fetch(5).wait()

        def mid(i):
            s = start[tile(i), :].astype(F32)
            up2 = col_ref[tile(i), 2:3] * signal
            up1 = up2 + dot(ci_ref[1, tile(i), :], hgrad1)
            gate1[tile(i), :] = up1 + gate1[tile(i), :] * up2 + gate0[tile(i), :] * up1
            low0[tile(i), :] = (s * up1).astype(BF)

        loop(mid)
        fetch(6).wait()
        hgrad0 = dot(co_ref[0], low0[...]).astype(BF)
        small[3] = hgrad0
        fetch(7).wait()

        def fin(i):
            low[tile(i), :] = (gate1[tile(i), :] + dot(ci_ref[0, tile(i), :], hgrad0)).astype(BF)

        loop(fin)
        for t, (first, count, kind, index) in enumerate(tables):
            grad = low[(t + 1) * PROJECTED : (t + 2) * PROJECTED, :]
            block = dot(ps[kind][index], grad).astype(BF)
            for k in range(count):
                back_ref[slot_ref[first + k]] = block[k * BLOCK_WIDTH : (k + 1) * BLOCK_WIDTH, :]

    return kernel


def make_grads(orders, splits, devices, chunk, chunk_pad):
    half = devices // 2
    colors = len(splits)

    def kernel(me_ref, start, layer1, low1, low0, small, *refs):
        los, his, acc = refs[:colors], refs[colors : 2 * colors], refs[2 * colors]
        group, rows = start.shape
        rank = small.shape[1]
        subs = group // chunk
        me = me_ref[0]
        acc[:, 0:rank] = dot(low1[...], small[1], NT)
        acc[:, rank : 2 * rank] = dot(layer1[...], small[2], NT)
        acc[:, 2 * rank : 3 * rank] = dot(low0[...], small[0], NT)
        acc[:, 3 * rank : 4 * rank] = dot(start[...], small[3], NT)
        ones = jnp.ones((8, rows), BF)
        biases = (dot(ones, low1[...], NT), dot(ones, low0[...], NT))
        spare = chunk_pad - chunk
        for s in range(subs):
            d = pl.program_id(0) * subs + s
            at = 0
            for which, cols in enumerate(splits):
                piece = acc[s * chunk : (s + 1) * chunk, at : at + cols]
                at += cols
                if which < 2:
                    tail = biases[which][0:spare, s * chunk : (s + 1) * chunk]
                    tail = jnp.concatenate([tail, jnp.zeros((spare, cols - chunk), F32)], 1)
                else:
                    tail = jnp.zeros((spare, cols), F32)
                value = jnp.concatenate([piece, tail], 0).astype(BF)
                place = position_of(d ^ me, orders[which])

                @pl.when(place < half)
                def _():
                    los[which][place] = value

                @pl.when(place >= half)
                def _():
                    his[which][place - half] = value

    return kernel


def add_pair(a, b):
    return (a.astype(F32) + b.astype(F32)).astype(BF)


def reduce_pieces(los, his, orders, devices):
    stages = len(orders[0])
    for k in range(stages):
        got = [
            lax.ppermute(h, AXES, [(i, i ^ o[k]) for i in range(devices)])
            for h, o in zip(his, orders)
        ]
        got = lax.optimization_barrier(got)
        if k == stages - 1:
            return [add_pair(a, b)[0] for a, b in zip(los, got)]
        n = los[0].shape[0] // 2
        his = [add_pair(a[n:], b[n:]) for a, b in zip(los, got)]
        los = [add_pair(a[:n], b[:n]) for a, b in zip(los, got)]


def body(
    pooled,
    slot_of_block,
    dense_part,
    labels,
    sample_weight,
    proj_wide,
    proj_mid,
    proj_narrow,
    cross_in,
    cross_out,
    cross_bias,
    head_weight,
):
    dp_count, rep_count = lax.axis_size("dp"), lax.axis_size("rep")
    devices = dp_count * rep_count
    rows = labels.shape[0]
    blocks_here = pooled.shape[1]
    width = cross_bias.shape[1]
    rank = cross_in.shape[2]
    chunk = width // devices
    chunk_pad = (chunk // 8 + 1) * 8

    core, masks = exchange_basis(dp_count, rep_count)
    last = masks[-1:]
    others = masks[:-1]
    colors = 3
    orders = [
        core + [others[(c + i) % len(others)] for i in range(len(others))] + last for c in range(colors)
    ]
    splits = [(4 * rank // LANES + colors - 1 - c) // colors * LANES for c in range(colors)]
    tables = []
    first = 0
    for kind, proj in enumerate((proj_wide, proj_mid, proj_narrow)):
        per = proj.shape[1] // BLOCK_WIDTH
        for index in range(proj.shape[0]):
            tables.append((first, per, kind, index))
            first += per

    received = lax.all_to_all(pack(pooled, sample_weight, devices), AXES, 0, 0, tiled=True)
    row_data = jnp.stack([sample_weight, labels.astype(F32)])
    col_data = jnp.stack([cross_bias[0], cross_bias[1], head_weight], 1)
    me = lax.axis_index(AXES).astype(jnp.int32).reshape(1)

    smem = pl.BlockSpec(memory_space=pltpu.SMEM)
    vmem = pl.BlockSpec(memory_space=pltpu.VMEM)
    hbm = pl.BlockSpec(memory_space=pl.ANY)
    wide = jax.ShapeDtypeStruct((width, rows), BF)
    back, start, layer1, low1, low0, small = pl.pallas_call(
        make_step(tables, devices, blocks_here),
        in_specs=[smem] + [vmem] * 10 + [hbm] * 4,
        out_specs=[vmem] * 6,
        out_shape=[
            jax.ShapeDtypeStruct((blocks_here * devices, BLOCK_WIDTH, rows), BF),
            wide,
            wide,
            wide,
            wide,
            jax.ShapeDtypeStruct((4, rank, rows), BF),
        ],
        scratch_shapes=[
            pltpu.VMEM((2, rank, width), BF),
            pltpu.VMEM((2, width, rank), BF),
            pltpu.VMEM((2, width, rank), BF),
            pltpu.VMEM((2, rank, width), BF),
            pltpu.VMEM((width, rows), BF),
            pltpu.VMEM((width, rows), F32),
            pltpu.VMEM((width, rows), F32),
            pltpu.SemaphoreType.DMA((8,)),
        ],
        compiler_params=pltpu.CompilerParams(vmem_limit_bytes=50 << 20),
        cost_estimate=pl.CostEstimate(flops=16 * width * rank * rows, bytes_accessed=20 << 20, transcendentals=rows),
        name="step",
    )(
        slot_of_block,
        received,
        dense_part,
        row_data,
        col_data,
        jnp.swapaxes(proj_wide, 1, 2),
        jnp.swapaxes(proj_mid, 1, 2),
        jnp.swapaxes(proj_narrow, 1, 2),
        proj_wide,
        proj_mid,
        proj_narrow,
        jnp.swapaxes(cross_in, 1, 2),
        cross_in,
        jnp.swapaxes(cross_out, 1, 2),
        cross_out,
    )
    back = back.reshape(devices, blocks_here * BLOCK_WIDTH, rows)
    back = lax.all_to_all(back, AXES, 0, 0, tiled=True)

    group = chunk
    while group % 16:
        group += chunk
    part = pl.BlockSpec((group, rows), lambda i: (i, 0))
    half = [jax.ShapeDtypeStruct((devices // 2, chunk_pad, c), BF) for c in splits]
    outs = pl.pallas_call(
        make_grads(orders, splits, devices, chunk, chunk_pad),
        grid=(width // group,),
        in_specs=[smem, part, part, part, part, pl.BlockSpec((4, rank, rows), lambda i: (0, 0, 0))],
        out_specs=[pl.BlockSpec(h.shape, lambda i: (0, 0, 0)) for h in half + half],
        out_shape=half + half,
        scratch_shapes=[pltpu.VMEM((group, 4 * rank), F32)],
        compiler_params=pltpu.CompilerParams(vmem_limit_bytes=32 << 20),
        cost_estimate=pl.CostEstimate(flops=8 * width * rank * rows, bytes_accessed=16 << 20, transcendentals=0),
        name="grads",
    )(me, start, layer1, low1, low0, small)
    sums = reduce_pieces(list(outs[:colors]), list(outs[colors:]), orders, devices)
    pooled_grad = unpack(back)
    bias1, bias0 = sums[0][chunk, :chunk], sums[1][chunk, :chunk]
    flat = jnp.concatenate([x[:chunk] for x in sums], 1)
    out1, in1, out0, in0 = [flat[:, i * rank : (i + 1) * rank] for i in range(4)]
    grad_in = jnp.stack([in0, in1]).astype(F32)
    grad_out = jnp.stack([out0.T, out1.T]).astype(F32)
    grad_bias = jnp.stack([bias0, bias1]).astype(F32)
    return (pooled_grad, grad_in, grad_out, grad_bias)


def solution(mesh):
    return jax.shard_map(
        body,
        mesh=mesh,
        in_specs=(
            P(None, AXES, None),
            P(),
            P(None, AXES),
            P(AXES),
            P(AXES),
            P(),
            P(),
            P(),
            P(),
            P(),
            P(),
            P(),
        ),
        out_specs=(
            P(None, AXES, None),
            P(None, AXES, None),
            P(None, None, AXES),
            P(None, AXES),
        ),
        check_vma=False,
    )
```

time: 437 us -> 148 us (0.34)
  waiting for transfers between devices: 189 us -> 51.1 us
  blocking collectives: 91.5 us -> 0 us
  local copies, waits for them, and re-layouts: 101 us -> 22.5 us
  Pallas kernels: 0 us -> 41.1 us
  matrix products: 22.5 us -> 0 us
  between operations: 15.2 us -> 0.96 us
  starting transfers between devices: 10.9 us -> 23.3 us
    unnamed x2 -> x0, waiting for transfers between devices: 165 us -> none
    unnamed x1 -> x0, blocking collectives: 91.5 us -> none
    pallas_call x0 -> x4, Pallas kernels: none -> 41.1 us  [the longest x1 20.9 us: body(): pl.pallas_call(make_step(tables, devices, blocks_here), in_specs=[smem] +...]
    ppermute x0 -> x15, waiting for transfers between devices: none -> 38.1 us  [reduce_pieces(): lax.ppermute(h, AXES, [(i, i ^ o[k]) for i in range(devices)])]
    concatenate x2 -> x0, local copies, waits for them, and re-layouts: 25.6 us -> none  [the longest x1 24.9 us: body(): weight_terms = jnp.concatenate([in_term, out_term], 0)]
    dot_general x19 -> x0, matrix products: 22.5 us -> none  [the longest x2 7.39 us: block_step(): jnp.einsum('wk,kr->wr', cross_in[layer], hidden_grad, preferred_element_t...]
    unnamed x49 -> x37, local copies, waits for them, and re-layouts: 41.3 us -> 19 us
    scatter x1 -> x0, local copies, waits for them, and re-layouts: 15.8 us -> none  [block_step(): jnp.zeros(logical_grad.shape, jnp.float32).at[:, slot_of_block, :]]
  transfers between devices with their start and end apart: 3 -> 17, of which waited for: 2 -> 6; matrix products, arithmetic and copies ran while one was open for 7% -> 13% of each run, Pallas kernels for 0% -> 4%
where the time goes in v1:
time: 148 us; the launch traced here: 147 us
  waiting for transfers between devices  51.1 us (35%)
  Pallas kernels  41.1 us (28%)
  starting transfers between devices  23.3 us (16%)
  local copies, waits for them, and re-layouts  22.5 us (15%)
  other arithmetic  7.78 us (5%)
    ppermute x15, waiting for transfers between devices, reduce_pieces(): lax.ppermute(h, AXES, [(i, i ^ o[k]) for i in range(devices)])  38.1 us
    pallas_call x1, Pallas kernels, body(): pl.pallas_call(make_step(tables, devices, blocks_here), in_specs=[smem] +...  20.9 us
    unnamed x37, local copies, waits for them, and re-layouts  19 us
    all_to_all x1, waiting for transfers between devices, body(): lax.all_to_all(pack(pooled, sample_weight, devices), AXES, 0, 0, tiled=True)  12.9 us
    ppermute x15, starting transfers between devices, reduce_pieces(): lax.ppermute(h, AXES, [(i, i ^ o[k]) for i in range(devices)])  12.9 us
    pallas_call x1, Pallas kernels, body(): pl.pallas_call(make_grads(orders, splits, devices, chunk, chunk_pad), gri...  8.43 us
    all_to_all x1, starting transfers between devices, body(): lax.all_to_all(pack(pooled, sample_weight, devices), AXES, 0, 0, tiled=True)  7.44 us
    convert_element_type x14, other arithmetic, add_pair(): return (a.astype(F32) + b.astype(F32)).astype(BF)  6.48 us
  transfers between devices with their start and end apart: 17, of which 6 were waited for; matrix products, arithmetic and copies ran while one was open for 13% of the time, Pallas kernels for 4%

profile of v1, /device:TPU:0, one launch (start us, length us, event | category | flops | bytes accessed | tf_op | source)
XLA Modules:
  0.0 146.7 jit_solution(11595623897612125573)
XLA Ops:
  0.6 5.9 %pack.1 = bf16[32,136,128]{2,1,0:T(8,128)(2,1)} custom-call(f32[2,128]{1,0:T(2,128)} %bitcast.37, bf16[16,4,8192]{2,1,0:T(4,128)(2,1)} %x_ref.1), custom_call_target="tpu_custom_call" | custom-call | tf_op jit(solution)/shard_map/pack/pallas_call | solution.py:85
  6.6 7.4 %all-to-all-start = ((bf16[32,136,128]{2,1,0:T(8,128)(2,1)}), bf16[32,136,128]{2,1,0:T(8,128)(2,1)}, u32[]{:S(2)}, u32[]{:S(2)}) async-start(bf16[32,136,128]{2,1,0:T(8,128)(2,1)} %pack.1), calls=%async_computation | async-start | bytes 2228224 | tf_op jit(solution)/shard_map/all_to_all | solution.py:372
  15.6 2.6 %copy.38.col_ref = f32[3456,3]{1,0:T(8,128)} copy(f32[3456,3]{0,1:T(4,128)} %pad_maximum_fusion.1) | data formatting | bytes 82944 | tf_op jit(solution)/shard_map/stack | solution.py:374
  18.2 3.7 %copy.36 = bf16[2,3456,256]{1,2,0:T(8,128)(2,1)} copy(bf16[2,3456,256]{2,1,0:T(8,128)(2,1)S(1)} %copy-done.9) | data formatting | bytes 7077888 | tf_op args[8]
  21.9 5.8 %copy.37 = bf16[2,256,3456]{1,2,0:T(8,128)(2,1)} copy(bf16[2,256,3456]{2,1,0:T(8,128)(2,1)} %co_hbm.1) | data formatting | bytes 7077888 | tf_op args[9]
  28.7 12.9 %all-to-all-done.x_ref = bf16[32,136,128]{2,1,0:T(8,128)(2,1)} async-done(((bf16[32,136,128]{2,1,0:T(8,128)(2,1)}), bf16[32,136,128]{2,1,0:T(8,128)(2,1)}, u32[]{:S(2)}, u32[]{:S(2)}) %all-to-all-start) | async-done | bytes 1114144 | tf_op jit(solution)/shard_map/all_to_all | solution.py:372
  41.6 20.9 %step.1 = (bf16[128,16,256]{2,1,0:T(8,128)(2,1)}, bf16[3456,256]{1,0:T(8,128)(2,1)}, bf16[3456,256]{1,0:T(8,128)(2,1)}, bf16[3456,256]{1,0:T(8,128)(2,1)}, bf16[...) custom-call(s32[128]{0:T(128)S(1)} %copy-done.8, bf16[32,136,128]{2,1,0:T(8,128)(2,1)} %all-to-all-done.x_ref, ...), custom_call_target="tpu_custom_call" | custom-call | flops 3623878656 | bytes 20971520 | tf_op jit(solution)/shard_map/step/pallas_call | solution.py:381
  64.1 1.5 %copy-done.1 = bf16[3456,256]{1,0:T(8,128)(2,1)S(1)} copy-done((bf16[3456,256]{1,0:T(8,128)(2,1)S(1)}, bf16[3456,256]{1,0:T(8,128)(2,1)}, u32[]{:S(2)}) %copy-start.1) | copy-done | bytes 1769496
  65.6 1.5 %copy-done.2 = bf16[3456,256]{1,0:T(8,128)(2,1)S(1)} copy-done((bf16[3456,256]{1,0:T(8,128)(2,1)S(1)}, bf16[3456,256]{1,0:T(8,128)(2,1)}, u32[]{:S(2)}) %copy-start.2) | copy-done | bytes 1769496
  67.0 1.5 %copy-done.3 = bf16[3456,256]{1,0:T(8,128)(2,1)S(1)} copy-done((bf16[3456,256]{1,0:T(8,128)(2,1)S(1)}, bf16[3456,256]{1,0:T(8,128)(2,1)}, u32[]{:S(2)}) %copy-start.3) | copy-done | bytes 1769496
  68.5 8.4 %grads.1 = (bf16[16,112,384]{2,1,0:T(8,128)(2,1)S(1)}, bf16[16,112,384]{2,1,0:T(8,128)(2,1)S(1)}, bf16[16,112,256]{2,1,0:T(8,128)(2,1)S(1)}, bf16[16,112,384]{2,...) custom-call(s32[1]{0:T(128)} %bitcast.11.me_ref, ...), custom_call_target="tpu_custom_call" | custom-call | flops 1811939328 | bytes 16777216 | tf_op jit(solution)/shard_map/grads/pallas_call | solution.py:431
  77.6 5.8 %collective-permute-done.2 = bf16[16,112,256]{2,1,0:T(8,128)(2,1)S(1)} collective-permute-done((bf16[16,112,256]{2,1,0:T(8,128)(2,1)S(1)}, bf16[16,112,256]{2,1,0:T(8,128)(2,1)S(1)}, u32[]{:S(2)}, u32[]{:S(2)}) %collective-permute-start.2) | collective-permute-done | bytes 917536 | tf_op jit(solution)/shard_map/ppermute | solution.py:322
  84.6 1.5 %collective-permute-start.4 = (bf16[8,112,384]{2,1,0:T(8,128)(2,1)}, bf16[8,112,384]{2,1,0:T(8,128)(2,1)}, u32[]{:S(2)}, u32[]{:S(2)}) collective-permute-start(bf16[8,112,384]{2,1,0:T(8,128)(2,1)} %get-tuple-element.71), channel_id=1, source_target_pairs={{0,4},{1,5},{2,6},{3,7},{4,0},{5,1},{6,2},{7,3},{8,12},{9,13},{10,... | collective-permute-start | bytes 2064392 | tf_op jit(solution)/shard_map/ppermute | solution.py:322
  87.4 1.5 %collective-permute-start.3 = (bf16[8,112,384]{2,1,0:T(8,128)(2,1)}, bf16[8,112,384]{2,1,0:T(8,128)(2,1)}, u32[]{:S(2)}, u32[]{:S(2)}) collective-permute-start(bf16[8,112,384]{2,1,0:T(8,128)(2,1)} %get-tuple-element.72), channel_id=1, source_target_pairs={{0,2},{1,3},{2,0},{3,1},{4,6},{5,7},{6,4},{7,5},{8,10},{9,11},{10,... | collective-permute-start | bytes 2064392 | tf_op jit(solution)/shard_map/ppermute | solution.py:322
  89.9 2.9 %all-to-all-start.1 = ((bf16[32,64,256]{2,1,0:T(8,128)(2,1)}), bf16[32,64,256]{2,1,0:T(8,128)(2,1)S(1)}, u32[]{:S(2)}, u32[]{:S(2)}) async-start(bf16[32,64,256]{2,1,0:T(8,128)(2,1)} %bitcast.10), calls=%async_computation.1 | async-start | bytes 2097152 | tf_op jit(solution)/shard_map/all_to_all | solution.py:424
  92.8 17.6 %collective-permute-done.5 = bf16[8,112,256]{2,1,0:T(8,128)(2,1)S(1)} collective-permute-done((bf16[8,112,256]{2,1,0:T(8,128)(2,1)}, bf16[8,112,256]{2,1,0:T(8,128)(2,1)S(1)}, u32[]{:S(2)}, u32[]{:S(2)}) %collective-permute-start.5) | collective-permute-done | bytes 458784 | tf_op jit(solution)/shard_map/ppermute | solution.py:322
  113.9 1.7 %collective-permute-start.8 = (bf16[4,112,256]{2,1,0:T(8,128)(2,1)S(1)}, bf16[4,112,256]{2,1,0:T(8,128)(2,1)S(1)}, u32[]{:S(2)}, u32[]{:S(2)}) collective-permute-start(bf16[4,112,256]{2,1,0:T(8,128)(2,1)S(1)} %get-tuple-element.81), channel_id=1, source_target_pairs={{0,2},{1,3},{2,0},{3,1},{4,6},{5,7},{6,4},{7,5},{8,10},{9,11},{10,... | collective-permute-start | bytes 688136 | tf_op jit(solution)/shard_map/ppermute | solution.py:322
  115.6 5.4 %collective-permute-done.8 = bf16[4,112,256]{2,1,0:T(8,128)(2,1)S(1)} collective-permute-done((bf16[4,112,256]{2,1,0:T(8,128)(2,1)S(1)}, bf16[4,112,256]{2,1,0:T(8,128)(2,1)S(1)}, u32[]{:S(2)}, u32[]{:S(2)}) %collective-permute-start.8) | collective-permute-done | bytes 229408 | tf_op jit(solution)/shard_map/ppermute | solution.py:322
  121.0 5.3 %collective-permute-done.7 = bf16[4,112,384]{2,1,0:T(8,128)(2,1)S(1)} collective-permute-done((bf16[4,112,384]{2,1,0:T(8,128)(2,1)S(1)}, bf16[4,112,384]{2,1,0:T(8,128)(2,1)S(1)}, u32[]{:S(2)}, u32[]{:S(2)}) %collective-permute-start.7) | collective-permute-done | bytes 344096 | tf_op jit(solution)/shard_map/ppermute | solution.py:322
  128.7 4.0 %collective-permute-done.11 = bf16[2,112,256]{2,1,0:T(8,128)(2,1)S(1)} collective-permute-done((bf16[2,112,256]{2,1,0:T(8,128)(2,1)S(1)}, bf16[2,112,256]{2,1,0:T(8,128)(2,1)S(1)}, u32[]{:S(2)}, u32[]{:S(2)}) %collective-permute-start.11) | collective-permute-done | bytes 114720 | tf_op jit(solution)/shard_map/ppermute | solution.py:322
  132.7 1.5 %collective-permute-start.13 = (bf16[1,112,384]{2,1,0:T(8,128)(2,1)S(1)}, bf16[1,112,384]{2,1,0:T(8,128)(2,1)S(1)}, u32[]{:S(2)}, u32[]{:S(2)}) collective-permute-start(bf16[1,112,384]{2,1,0:T(8,128)(2,1)S(1)} %add_convert_fusion.22), channel_id=1, source_target_pairs={{0,16},{1,17},{2,18},{3,19},{4,20},{5,21},{6,22},{7,23},{8,24},{9,... | collective-permute-start | bytes 258056 | tf_op jit(solution)/shard_map/ppermute | solution.py:322
  134.3 1.5 %collective-permute-start.12 = (bf16[1,112,384]{2,1,0:T(8,128)(2,1)S(1)}, bf16[1,112,384]{2,1,0:T(8,128)(2,1)S(1)}, u32[]{:S(2)}, u32[]{:S(2)}) collective-permute-start(bf16[1,112,384]{2,1,0:T(8,128)(2,1)S(1)} %add_convert_fusion.23), channel_id=1, source_target_pairs={{0,16},{1,17},{2,18},{3,19},{4,20},{5,21},{6,22},{7,23},{8,24},{9,... | collective-permute-start | bytes 258056 | tf_op jit(solution)/shard_map/ppermute | solution.py:322
  135.8 1.5 %collective-permute-start.14 = (bf16[1,112,256]{2,1,0:T(8,128)(2,1)S(1)}, bf16[1,112,256]{2,1,0:T(8,128)(2,1)S(1)}, u32[]{:S(2)}, u32[]{:S(2)}) collective-permute-start(bf16[1,112,256]{2,1,0:T(8,128)(2,1)S(1)} %add_convert_fusion.25), channel_id=1, source_target_pairs={{0,16},{1,17},{2,18},{3,19},{4,20},{5,21},{6,22},{7,23},{8,24},{9,... | collective-permute-start | bytes 172040 | tf_op jit(solution)/shard_map/ppermute | solution.py:322
  138.3 5.8 %unpack.1 = f32[16,4,8192]{2,1,0:T(4,128)} custom-call(bf16[32,64,256]{2,1,0:T(8,128)(2,1)} %copy-done.10), custom_call_target="tpu_custom_call" | custom-call | tf_op jit(solution)/shard_map/unpack/pallas_call | solution.py:116
  (82 shorter events, 17.5 us)
Async XLA Ops:
  0.6 13.4 %copy-start.12 = (f32[3456]{0:T(1024)S(1)}, f32[3456]{0:T(1024)}, u32[]{:S(2)}) copy-start(f32[3456]{0:T(1024)} %param.23) | copy-start | bytes 41476
  6.6 11.6 %copy-start.9 = (bf16[2,3456,256]{2,1,0:T(8,128)(2,1)S(1)}, bf16[2,3456,256]{2,1,0:T(8,128)(2,1)}, u32[]{:S(2)}) copy-start(bf16[2,3456,256]{2,1,0:T(8,128)(2,1)} %ci_hbm.1) | copy-start | bytes 10616836
  6.6 35.0 %all-to-all-start = ((bf16[32,136,128]{2,1,0:T(8,128)(2,1)}), bf16[32,136,128]{2,1,0:T(8,128)(2,1)}, u32[]{:S(2)}, u32[]{:S(2)}) async-start(bf16[32,136,128]{2,1,0:T(8,128)(2,1)} %pack.1), calls=%async_computation | async-start | bytes 2228224 | tf_op jit(solution)/shard_map/all_to_all | solution.py:372
  21.9 5.8 %copy-start.6 = (bf16[16,16,128]{2,1,0:T(8,128)(2,1)S(1)}, bf16[16,16,128]{2,1,0:T(8,128)(2,1)}, u32[]{:S(2)}) copy-start(bf16[16,16,128]{2,1,0:T(8,128)(2,1)} %p2.1) | copy-start | bytes 196612
  21.9 6.1 %copy-start.4 = (bf16[6,256,128]{2,1,0:T(8,128)(2,1)S(1)}, bf16[6,256,128]{2,1,0:T(8,128)(2,1)}, u32[]{:S(2)}) copy-start(bf16[6,256,128]{2,1,0:T(8,128)(2,1)} %p0.1) | copy-start | bytes 1179652
  27.7 14.0 %copy-start.7 = (bf16[128,256]{1,0:T(8,128)(2,1)S(1)}, bf16[128,256]{1,0:T(8,128)(2,1)}, u32[]{:S(2)}) copy-start(bf16[128,256]{1,0:T(8,128)(2,1)} %dense_ref.1) | copy-start | bytes 196612
  27.7 13.9 %copy-start.8 = (s32[128]{0:T(128)S(1)}, s32[128]{0:T(128)}, u32[]{:S(2)}) copy-start(s32[128]{0:T(128)} %slot_ref.1) | copy-start | bytes 1540
  76.9 6.5 %collective-permute-start = (bf16[16,112,384]{2,1,0:T(8,128)(2,1)S(1)}, bf16[16,112,384]{2,1,0:T(8,128)(2,1)S(1)}, u32[]{:S(2)}, u32[]{:S(2)}) collective-permute-start(bf16[16,112,384]{2,1,0:T(8,128)(2,1)S(1)} %get-tuple-element.38), channel_id=1, source_target_pairs={{0,1},{1,0},{2,3},{3,2},{4,5},{5,4},{6,7},{7,6},{8,9},{9,8},{10,11... | collective-permute-start | bytes 4128776 | tf_op jit(solution)/shard_map/ppermute | solution.py:322
  77.0 6.4 %collective-permute-start.1 = (bf16[16,112,384]{2,1,0:T(8,128)(2,1)S(1)}, bf16[16,112,384]{2,1,0:T(8,128)(2,1)S(1)}, u32[]{:S(2)}, u32[]{:S(2)}) collective-permute-start(bf16[16,112,384]{2,1,0:T(8,128)(2,1)S(1)} %get-tuple-element.39), channel_id=1, source_target_pairs={{0,1},{1,0},{2,3},{3,2},{4,5},{5,4},{6,7},{7,6},{8,9},{9,8},{10,11... | collective-permute-start | bytes 4128776 | tf_op jit(solution)/shard_map/ppermute | solution.py:322
  77.5 5.9 %collective-permute-start.2 = (bf16[16,112,256]{2,1,0:T(8,128)(2,1)S(1)}, bf16[16,112,256]{2,1,0:T(8,128)(2,1)S(1)}, u32[]{:S(2)}, u32[]{:S(2)}) collective-permute-start(bf16[16,112,256]{2,1,0:T(8,128)(2,1)S(1)} %get-tuple-element.40), channel_id=1, source_target_pairs={{0,1},{1,0},{2,3},{3,2},{4,5},{5,4},{6,7},{7,6},{8,9},{9,8},{10,11... | collective-permute-start | bytes 2752520 | tf_op jit(solution)/shard_map/ppermute | solution.py:322
  84.6 25.8 %collective-permute-start.4 = (bf16[8,112,384]{2,1,0:T(8,128)(2,1)}, bf16[8,112,384]{2,1,0:T(8,128)(2,1)}, u32[]{:S(2)}, u32[]{:S(2)}) collective-permute-start(bf16[8,112,384]{2,1,0:T(8,128)(2,1)} %get-tuple-element.71), channel_id=1, source_target_pairs={{0,4},{1,5},{2,6},{3,7},{4,0},{5,1},{6,2},{7,3},{8,12},{9,13},{10,... | collective-permute-start | bytes 2064392 | tf_op jit(solution)/shard_map/ppermute | solution.py:322
  87.4 23.0 %collective-permute-start.3 = (bf16[8,112,384]{2,1,0:T(8,128)(2,1)}, bf16[8,112,384]{2,1,0:T(8,128)(2,1)}, u32[]{:S(2)}, u32[]{:S(2)}) collective-permute-start(bf16[8,112,384]{2,1,0:T(8,128)(2,1)} %get-tuple-element.72), channel_id=1, source_target_pairs={{0,2},{1,3},{2,0},{3,1},{4,6},{5,7},{6,4},{7,5},{8,10},{9,11},{10,... | collective-permute-start | bytes 2064392 | tf_op jit(solution)/shard_map/ppermute | solution.py:322
  89.9 20.5 %collective-permute-start.5 = (bf16[8,112,256]{2,1,0:T(8,128)(2,1)}, bf16[8,112,256]{2,1,0:T(8,128)(2,1)S(1)}, u32[]{:S(2)}, u32[]{:S(2)}) collective-permute-start(bf16[8,112,256]{2,1,0:T(8,128)(2,1)} %get-tuple-element.75), channel_id=1, source_target_pairs={{0,8},{1,9},{2,10},{3,11},{4,12},{5,13},{6,14},{7,15},{8,0},{9,1},... | collective-permute-start | bytes 1376264 | tf_op jit(solution)/shard_map/ppermute | solution.py:322
  89.9 47.5 %all-to-all-start.1 = ((bf16[32,64,256]{2,1,0:T(8,128)(2,1)}), bf16[32,64,256]{2,1,0:T(8,128)(2,1)S(1)}, u32[]{:S(2)}, u32[]{:S(2)}) async-start(bf16[32,64,256]{2,1,0:T(8,128)(2,1)} %bitcast.10), calls=%async_computation.1 | async-start | bytes 2097152 | tf_op jit(solution)/shard_map/all_to_all | solution.py:424
  111.7 14.6 %collective-permute-start.7 = (bf16[4,112,384]{2,1,0:T(8,128)(2,1)S(1)}, bf16[4,112,384]{2,1,0:T(8,128)(2,1)S(1)}, u32[]{:S(2)}, u32[]{:S(2)}) collective-permute-start(bf16[4,112,384]{2,1,0:T(8,128)(2,1)S(1)} %get-tuple-element.77), channel_id=1, source_target_pairs={{0,8},{1,9},{2,10},{3,11},{4,12},{5,13},{6,14},{7,15},{8,0},{9,1},... | collective-permute-start | bytes 1032200 | tf_op jit(solution)/shard_map/ppermute | solution.py:322
  113.3 13.0 %collective-permute-start.6 = (bf16[4,112,384]{2,1,0:T(8,128)(2,1)S(1)}, bf16[4,112,384]{2,1,0:T(8,128)(2,1)S(1)}, u32[]{:S(2)}, u32[]{:S(2)}) collective-permute-start(bf16[4,112,384]{2,1,0:T(8,128)(2,1)S(1)} %get-tuple-element.78), channel_id=1, source_target_pairs={{0,4},{1,5},{2,6},{3,7},{4,0},{5,1},{6,2},{7,3},{8,12},{9,13},{10,... | collective-permute-start | bytes 1032200 | tf_op jit(solution)/shard_map/ppermute | solution.py:322
  113.9 7.1 %collective-permute-start.8 = (bf16[4,112,256]{2,1,0:T(8,128)(2,1)S(1)}, bf16[4,112,256]{2,1,0:T(8,128)(2,1)S(1)}, u32[]{:S(2)}, u32[]{:S(2)}) collective-permute-start(bf16[4,112,256]{2,1,0:T(8,128)(2,1)S(1)} %get-tuple-element.81), channel_id=1, source_target_pairs={{0,2},{1,3},{2,0},{3,1},{4,6},{5,7},{6,4},{7,5},{8,10},{9,11},{10,... | collective-permute-start | bytes 688136 | tf_op jit(solution)/shard_map/ppermute | solution.py:322
  126.4 6.2 %collective-permute-start.10 = (bf16[2,112,384]{2,1,0:T(8,128)(2,1)S(1)}, bf16[2,112,384]{2,1,0:T(8,128)(2,1)S(1)}, u32[]{:S(2)}, u32[]{:S(2)}) collective-permute-start(bf16[2,112,384]{2,1,0:T(8,128)(2,1)S(1)} %get-tuple-element.83), channel_id=1, source_target_pairs={{0,2},{1,3},{2,0},{3,1},{4,6},{5,7},{6,4},{7,5},{8,10},{9,11},{10,... | collective-permute-start | bytes 516104 | tf_op jit(solution)/shard_map/ppermute | solution.py:322
  127.1 5.5 %collective-permute-start.9 = (bf16[2,112,384]{2,1,0:T(8,128)(2,1)S(1)}, bf16[2,112,384]{2,1,0:T(8,128)(2,1)S(1)}, u32[]{:S(2)}, u32[]{:S(2)}) collective-permute-start(bf16[2,112,384]{2,1,0:T(8,128)(2,1)S(1)} %get-tuple-element.84), channel_id=1, source_target_pairs={{0,8},{1,9},{2,10},{3,11},{4,12},{5,13},{6,14},{7,15},{8,0},{9,1},... | collective-permute-start | bytes 516104 | tf_op jit(solution)/shard_map/ppermute | solution.py:322
  127.8 4.9 %collective-permute-start.11 = (bf16[2,112,256]{2,1,0:T(8,128)(2,1)S(1)}, bf16[2,112,256]{2,1,0:T(8,128)(2,1)S(1)}, u32[]{:S(2)}, u32[]{:S(2)}) collective-permute-start(bf16[2,112,256]{2,1,0:T(8,128)(2,1)S(1)} %get-tuple-element.87), channel_id=1, source_target_pairs={{0,4},{1,5},{2,6},{3,7},{4,0},{5,1},{6,2},{7,3},{8,12},{9,13},{10,... | collective-permute-start | bytes 344072 | tf_op jit(solution)/shard_map/ppermute | solution.py:322
  132.6 11.5 %copy-start.11 = (bf16[2,112,256]{2,1,0:T(8,128)(2,1)}, bf16[2,112,256]{2,1,0:T(8,128)(2,1)S(1)}, u32[]{:S(2)}) copy-start(bf16[2,112,256]{2,1,0:T(8,128)(2,1)S(1)} %collective-permute-done.11) | copy-start | bytes 344068
  132.7 11.5 %collective-permute-start.13 = (bf16[1,112,384]{2,1,0:T(8,128)(2,1)S(1)}, bf16[1,112,384]{2,1,0:T(8,128)(2,1)S(1)}, u32[]{:S(2)}, u32[]{:S(2)}) collective-permute-start(bf16[1,112,384]{2,1,0:T(8,128)(2,1)S(1)} %add_convert_fusion.22), channel_id=1, source_target_pairs={{0,16},{1,17},{2,18},{3,19},{4,20},{5,21},{6,22},{7,23},{8,24},{9,... | collective-permute-start | bytes 258056 | tf_op jit(solution)/shard_map/ppermute | solution.py:322
  134.3 9.9 %collective-permute-start.12 = (bf16[1,112,384]{2,1,0:T(8,128)(2,1)S(1)}, bf16[1,112,384]{2,1,0:T(8,128)(2,1)S(1)}, u32[]{:S(2)}, u32[]{:S(2)}) collective-permute-start(bf16[1,112,384]{2,1,0:T(8,128)(2,1)S(1)} %add_convert_fusion.23), channel_id=1, source_target_pairs={{0,16},{1,17},{2,18},{3,19},{4,20},{5,21},{6,22},{7,23},{8,24},{9,... | collective-permute-start | bytes 258056 | tf_op jit(solution)/shard_map/ppermute | solution.py:322
  135.8 8.3 %collective-permute-start.14 = (bf16[1,112,256]{2,1,0:T(8,128)(2,1)S(1)}, bf16[1,112,256]{2,1,0:T(8,128)(2,1)S(1)}, u32[]{:S(2)}, u32[]{:S(2)}) collective-permute-start(bf16[1,112,256]{2,1,0:T(8,128)(2,1)S(1)} %add_convert_fusion.25), channel_id=1, source_target_pairs={{0,16},{1,17},{2,18},{3,19},{4,20},{5,21},{6,22},{7,23},{8,24},{9,... | collective-permute-start | bytes 172040 | tf_op jit(solution)/shard_map/ppermute | solution.py:322
  (9 other events, 10.8 us)

commit v2 on v1

--- a/solution.py
+++ b/solution.py
@@ -80,7 +80,7 @@
     width, blocks, batch = pooled.shape
     rows = batch // devices
     per = rows // LANES
-    group = 4
+    group = 16
     depth = blocks * per * width + 8
     return pl.pallas_call(
         pack_kernel,
@@ -112,7 +112,7 @@
     width = BLOCK_WIDTH
     devices, both, rows = received.shape
     blocks = both // width
-    group = 4
+    group = 8
     return pl.pallas_call(
         unpack_kernel,
         grid=(devices // group,),
@@ -142,11 +142,15 @@
         cot_hbm,
         co_hbm,
         back_ref,
+        start_hbm,
+        layer1_hbm,
+        low1_hbm,
+        low0_hbm,
+        small,
         start,
         layer1,
         low1,
         low0,
-        small,
         cit_ref,
         ci_ref,
         cot_ref,
@@ -155,6 +159,7 @@
         gate0,
         gate1,
         sems,
+        out_sems,
     ):
         pts, ps = (pt0, pt1, pt2), (p0, p1, p2)
         width, rows = start.shape
@@ -172,15 +177,20 @@
 
         for n in range(len(uses)):
             fetch(n).start()
+        written = ((start, start_hbm), (layer1, layer1_hbm), (low1, low1_hbm), (low0, low0_hbm))
+
+        def save(n):
+            source, target = written[n]
+            return pltpu.make_async_copy(source, target, out_sems.at[n])
 
         def tile(i):
             return pl.ds(pl.multiple_of(i * tile_rows, tile_rows), tile_rows)
 
         def loop(body, init=None):
             if init is None:
-                lax.fori_loop(0, tiles, lambda i, c: (body(i), c)[1], 0)
+                lax.fori_loop(0, tiles, lambda i, c: (body(i), c)[1], 0, unroll=True)
                 return None
-            return lax.fori_loop(0, tiles, body, init)
+            return lax.fori_loop(0, tiles, body, init, unroll=True)
 
         start[0:PROJECTED, :] = dense_ref[...]
         for t, (first, count, kind, index) in enumerate(tables):
@@ -196,6 +206,8 @@
             block = parts[0] if count == 1 else jnp.concatenate(parts, 0)
             start[(t + 1) * PROJECTED : (t + 2) * PROJECTED, :] = dot(pts[kind][index], block).astype(BF)
 
+        save(0).start()
+
         fetch(0).wait()
         hidden0 = dot(cit_ref[0], start[...]).astype(BF)
         small[0] = hidden0
@@ -208,6 +220,7 @@
             layer1[tile(i), :] = (s * g + s).astype(BF)
 
         loop(fwd0)
+        save(1).start()
         fetch(2).wait()
         hidden1 = dot(cit_ref[1], layer1[...]).astype(BF)
         small[1] = hidden1
@@ -228,7 +241,7 @@
         def gather_total(d, carry):
             return carry + x_ref[d][depth - 8 : depth, :].astype(F32)
 
-        terms = lax.fori_loop(0, devices, gather_total, jnp.zeros((8, LANES), F32))
+        terms = lax.fori_loop(0, devices, gather_total, jnp.zeros((8, LANES), F32), unroll=8)
         total = jnp.sum(terms, 0, keepdims=True)[:, 0:1]
         scale = float(rows * devices) / total
         signal = scale * row_ref[0:1, :] * (jax.nn.sigmoid(logit) - row_ref[1:2, :])
@@ -238,6 +251,7 @@
             low1[tile(i), :] = (s * (col_ref[tile(i), 2:3] * signal)).astype(BF)
 
         loop(bwd1)
+        save(2).start()
         fetch(4).wait()
         hgrad1 = dot(co_ref[1], low1[...]).astype(BF)
         small[2] = hgrad1
@@ -251,6 +265,7 @@
             low0[tile(i), :] = (s * up1).astype(BF)
 
         loop(mid)
+        save(3).start()
         fetch(6).wait()
         hgrad0 = dot(co_ref[0], low0[...]).astype(BF)
         small[3] = hgrad0
@@ -265,6 +280,8 @@
             block = dot(ps[kind][index], grad).astype(BF)
             for k in range(count):
                 back_ref[slot_ref[first + k]] = block[k * BLOCK_WIDTH : (k + 1) * BLOCK_WIDTH, :]
+        for n in range(len(written)):
+            save(n).wait()
 
     return kernel
 
@@ -322,7 +339,8 @@
             lax.ppermute(h, AXES, [(i, i ^ o[k]) for i in range(devices)])
             for h, o in zip(his, orders)
         ]
-        got = lax.optimization_barrier(got)
+        if k:
+            got = lax.optimization_barrier(got)
         if k == stages - 1:
             return [add_pair(a, b)[0] for a, b in zip(los, got)]
         n = los[0].shape[0] // 2
@@ -330,7 +348,7 @@
         los = [add_pair(a[:n], b[:n]) for a, b in zip(los, got)]
 
 
-def body(
+def run(
     pooled,
     slot_of_block,
     dense_part,
@@ -381,7 +399,7 @@
     back, start, layer1, low1, low0, small = pl.pallas_call(
         make_step(tables, devices, blocks_here),
         in_specs=[smem] + [vmem] * 10 + [hbm] * 4,
-        out_specs=[vmem] * 6,
+        out_specs=[vmem] + [hbm] * 4 + [vmem],
         out_shape=[
             jax.ShapeDtypeStruct((blocks_here * devices, BLOCK_WIDTH, rows), BF),
             wide,
@@ -390,7 +408,8 @@
             wide,
             jax.ShapeDtypeStruct((4, rank, rows), BF),
         ],
-        scratch_shapes=[
+        scratch_shapes=[pltpu.VMEM((width, rows), BF)] * 4
+        + [
             pltpu.VMEM((2, rank, width), BF),
             pltpu.VMEM((2, width, rank), BF),
             pltpu.VMEM((2, width, rank), BF),
@@ -399,8 +418,9 @@
             pltpu.VMEM((width, rows), F32),
             pltpu.VMEM((width, rows), F32),
             pltpu.SemaphoreType.DMA((8,)),
+            pltpu.SemaphoreType.DMA((4,)),
         ],
-        compiler_params=pltpu.CompilerParams(vmem_limit_bytes=50 << 20),
+        compiler_params=pltpu.CompilerParams(vmem_limit_bytes=60 << 20),
         cost_estimate=pl.CostEstimate(flops=16 * width * rank * rows, bytes_accessed=20 << 20, transcendentals=rows),
         name="step",
     )(
@@ -426,6 +446,8 @@
     group = chunk
     while group % 16:
         group += chunk
+    if width % (2 * group) == 0:
+        group *= 2
     part = pl.BlockSpec((group, rows), lambda i: (i, 0))
     half = [jax.ShapeDtypeStruct((devices // 2, chunk_pad, c), BF) for c in splits]
     outs = pl.pallas_call(
@@ -435,11 +457,12 @@
         out_specs=[pl.BlockSpec(h.shape, lambda i: (0, 0, 0)) for h in half + half],
         out_shape=half + half,
         scratch_shapes=[pltpu.VMEM((group, 4 * rank), F32)],
-        compiler_params=pltpu.CompilerParams(vmem_limit_bytes=32 << 20),
+        compiler_params=pltpu.CompilerParams(vmem_limit_bytes=60 << 20),
         cost_estimate=pl.CostEstimate(flops=8 * width * rank * rows, bytes_accessed=16 << 20, transcendentals=0),
         name="grads",
     )(me, start, layer1, low1, low0, small)
-    sums = reduce_pieces(list(outs[:colors]), list(outs[colors:]), orders, devices)
+    los, his = list(outs[:colors]), list(outs[colors:])
+    sums = reduce_pieces(los, his, orders, devices)
     pooled_grad = unpack(back)
     bias1, bias0 = sums[0][chunk, :chunk], sums[1][chunk, :chunk]
     flat = jnp.concatenate([x[:chunk] for x in sums], 1)
@@ -452,7 +475,7 @@
 
 def solution(mesh):
     return jax.shard_map(
-        body,
+        run,
         mesh=mesh,
         in_specs=(
             P(None, AXES, None),

time: 148 us -> 137 us (0.926)
  waiting for transfers between devices: 51.1 us -> 46.9 us
  local copies, waits for them, and re-layouts: 22.5 us -> 18.5 us
  Pallas kernels: 41.1 us -> 37.2 us
  other arithmetic: 7.78 us -> 9.77 us
    unnamed x37 -> x29, local copies, waits for them, and re-layouts: 19 us -> 15 us
    pallas_call x1, Pallas kernels: 5.94 us -> 3.17 us  [pack(): pl.pallas_call(pack_kernel, grid=(devices // group,), in_specs=[pl.BlockS...]
    all_to_all x2, waiting for transfers between devices: 12.9 us -> 10.6 us  [the longest x1 10.6 us: run(): lax.all_to_all(pack(pooled, sample_weight, devices), AXES, 0, 0, tiled=True)]
    pallas_call x1, Pallas kernels: 5.77 us -> 3.95 us  [unpack(): pl.pallas_call(unpack_kernel, grid=(devices // group,), in_specs=[pl.Bloc...]
    ppermute x15, waiting for transfers between devices: 38.1 us -> 36.3 us  [reduce_pieces(): lax.ppermute(h, AXES, [(i, i ^ o[k]) for i in range(devices)])]
  transfers between devices with their start and end apart: 17 -> 17, of which waited for: 6 -> 7; matrix products, arithmetic and copies ran while one was open for 13% -> 18% of each run, Pallas kernels for 4% -> 3%
where the time goes in v2:
time: 137 us; the launch traced here: 136 us
  waiting for transfers between devices  46.9 us (34%)
  Pallas kernels  37.2 us (27%)
  starting transfers between devices  23.2 us (17%)
  local copies, waits for them, and re-layouts  18.5 us (14%)
  other arithmetic  9.77 us (7%)
    ppermute x15, waiting for transfers between devices, reduce_pieces(): lax.ppermute(h, AXES, [(i, i ^ o[k]) for i in range(devices)])  36.3 us
    pallas_call x1, Pallas kernels, run(): pl.pallas_call(make_step(tables, devices, blocks_here), in_specs=[smem] +...  16.9 us
    unnamed x29, local copies, waits for them, and re-layouts  15 us
    pallas_call x1, Pallas kernels, run(): pl.pallas_call(make_grads(orders, splits, devices, chunk, chunk_pad), gri...  13.1 us
    ppermute x15, starting transfers between devices, reduce_pieces(): lax.ppermute(h, AXES, [(i, i ^ o[k]) for i in range(devices)])  12.8 us
    all_to_all x1, waiting for transfers between devices, run(): lax.all_to_all(pack(pooled, sample_weight, devices), AXES, 0, 0, tiled=True)  10.6 us
    convert_element_type x14, other arithmetic, add_pair(): return (a.astype(F32) + b.astype(F32)).astype(BF)  7.89 us
    all_to_all x1, starting transfers between devices, run(): lax.all_to_all(pack(pooled, sample_weight, devices), AXES, 0, 0, tiled=True)  7.44 us
  transfers between devices with their start and end apart: 17, of which 7 were waited for; matrix products, arithmetic and copies ran while one was open for 18% of the time, Pallas kernels for 3%

profile of v2, /device:TPU:0, one launch (start us, length us, event | category | flops | bytes accessed | tf_op | source)
XLA Modules:
  0.0 136.4 jit_solution(11559722902868909765)
XLA Ops:
  0.6 3.2 %pack.1 = bf16[32,136,128]{2,1,0:T(8,128)(2,1)} custom-call(f32[2,128]{1,0:T(2,128)} %bitcast.38, bf16[16,4,8192]{2,1,0:T(4,128)(2,1)} %x_ref.1), custom_call_target="tpu_custom_call" | custom-call | tf_op jit(solution)/shard_map/pack/pallas_call | solution.py:85
  3.8 7.4 %all-to-all-start = ((bf16[32,136,128]{2,1,0:T(8,128)(2,1)}), bf16[32,136,128]{2,1,0:T(8,128)(2,1)}, u32[]{:S(2)}, u32[]{:S(2)}) async-start(bf16[32,136,128]{2,1,0:T(8,128)(2,1)} %pack.1), calls=%async_computation | async-start | bytes 2228224 | tf_op jit(solution)/shard_map/all_to_all | solution.py:390
  12.8 2.6 %copy.38.col_ref = f32[3456,3]{1,0:T(8,128)} copy(f32[3456,3]{0,1:T(4,128)} %pad_maximum_fusion.1) | data formatting | bytes 82944 | tf_op jit(solution)/shard_map/stack | solution.py:392
  15.4 3.7 %copy.36 = bf16[2,3456,256]{1,2,0:T(8,128)(2,1)} copy(bf16[2,3456,256]{2,1,0:T(8,128)(2,1)S(1)} %copy-done) | data formatting | bytes 7077888 | tf_op args[8]
  19.1 5.8 %copy.37 = bf16[2,256,3456]{1,2,0:T(8,128)(2,1)} copy(bf16[2,256,3456]{2,1,0:T(8,128)(2,1)} %co_hbm.1) | data formatting | bytes 7077888 | tf_op args[9]
  28.2 10.6 %all-to-all-done.x_ref = bf16[32,136,128]{2,1,0:T(8,128)(2,1)} async-done(((bf16[32,136,128]{2,1,0:T(8,128)(2,1)}), bf16[32,136,128]{2,1,0:T(8,128)(2,1)}, u32[]{:S(2)}, u32[]{:S(2)}) %all-to-all-start) | async-done | bytes 1114144 | tf_op jit(solution)/shard_map/all_to_all | solution.py:390
  38.9 16.9 %step.1 = (bf16[128,16,256]{2,1,0:T(8,128)(2,1)}, bf16[3456,256]{1,0:T(8,128)(2,1)}, bf16[3456,256]{1,0:T(8,128)(2,1)}, bf16[3456,256]{1,0:T(8,128)(2,1)}, bf16[...) custom-call(s32[128]{0:T(128)} %slot_ref.1, bf16[32,136,128]{2,1,0:T(8,128)(2,1)} %all-to-all-done.x_ref, ...), custom_call_target="tpu_custom_call" | custom-call | flops 3623878656 | bytes 20971520 | tf_op jit(solution)/shard_map/step/pallas_call | solution.py:399
  55.8 13.1 %grads.1 = (bf16[16,112,384]{2,1,0:T(8,128)(2,1)}, bf16[16,112,384]{2,1,0:T(8,128)(2,1)}, bf16[16,112,256]{2,1,0:T(8,128)(2,1)}, bf16[16,112,384]{2,1,0:T(8,128)...) custom-call(s32[1]{0:T(128)} %bitcast.11.me_ref, bf16[3456,256]{1,0:T(8,128)(2,1)} %get-tuple-element.29.start, ...), custom_call_target="tpu_custom_call" | custom-call | flops 1811939328 | bytes 16777216 | tf_op jit(solution)/shard_map/grads/pallas_call | solution.py:453
  69.5 2.8 %collective-permute-done.3 = bf16[16,112,384]{2,1,0:T(8,128)(2,1)S(1)} collective-permute-done((bf16[16,112,384]{2,1,0:T(8,128)(2,1)}, bf16[16,112,384]{2,1,0:T(8,128)(2,1)S(1)}, u32[]{:S(2)}, u32[]{:S(2)}) %collective-permute-start.3) | collective-permute-done | bytes 1376288 | tf_op jit(solution)/shard_map/ppermute | solution.py:339
  72.3 2.6 %add_convert_fusion = (bf16[8,112,384]{2,1,0:T(8,128)(2,1)S(1)}, bf16[8,112,384]{2,1,0:T(8,128)(2,1)}) fusion(bf16[16,112,384]{2,1,0:T(8,128)(2,1)S(1)} %collective-permute-done.3, bf16[16,112,384]{2,1,0:T(8,128)(2,1)} %get-tuple-element.38), kind=kLoop, calls=%fused_computation | loop fusion | flops 2752512 | bytes 4128768 | tf_op jit(solution)/shard_map/convert_element_type | solution.py:332
  74.9 1.5 %collective-permute-start.4 = (bf16[8,112,384]{2,1,0:T(8,128)(2,1)}, bf16[8,112,384]{2,1,0:T(8,128)(2,1)}, u32[]{:S(2)}, u32[]{:S(2)}) collective-permute-start(bf16[8,112,384]{2,1,0:T(8,128)(2,1)} %get-tuple-element.65), channel_id=1, source_target_pairs={{0,4},{1,5},{2,6},{3,7},{4,0},{5,1},{6,2},{7,3},{8,12},{9,13},{10,... | collective-permute-start | bytes 2064392 | tf_op jit(solution)/shard_map/ppermute | solution.py:339
  77.6 1.5 %collective-permute-start.2 = (bf16[8,112,384]{2,1,0:T(8,128)(2,1)}, bf16[8,112,384]{2,1,0:T(8,128)(2,1)}, u32[]{:S(2)}, u32[]{:S(2)}) collective-permute-start(bf16[8,112,384]{2,1,0:T(8,128)(2,1)} %get-tuple-element.66), channel_id=1, source_target_pairs={{0,2},{1,3},{2,0},{3,1},{4,6},{5,7},{6,4},{7,5},{8,10},{9,11},{10,... | collective-permute-start | bytes 2064392 | tf_op jit(solution)/shard_map/ppermute | solution.py:339
  80.1 2.9 %all-to-all-start.1 = ((bf16[32,64,256]{2,1,0:T(8,128)(2,1)}), bf16[32,64,256]{2,1,0:T(8,128)(2,1)S(1)}, u32[]{:S(2)}, u32[]{:S(2)}) async-start(bf16[32,64,256]{2,1,0:T(8,128)(2,1)} %bitcast.34), calls=%async_computation.1 | async-start | bytes 2097152 | tf_op jit(solution)/shard_map/all_to_all | solution.py:444
  83.0 17.6 %collective-permute-done.5 = bf16[8,112,256]{2,1,0:T(8,128)(2,1)S(1)} collective-permute-done((bf16[8,112,256]{2,1,0:T(8,128)(2,1)}, bf16[8,112,256]{2,1,0:T(8,128)(2,1)S(1)}, u32[]{:S(2)}, u32[]{:S(2)}) %collective-permute-start.5) | collective-permute-done | bytes 458784 | tf_op jit(solution)/shard_map/ppermute | solution.py:339
  100.7 1.3 add_convert_fusion.6
  102.3 1.3 add_convert_fusion.9
  104.1 1.7 %collective-permute-start.8 = (bf16[4,112,256]{2,1,0:T(8,128)(2,1)S(1)}, bf16[4,112,256]{2,1,0:T(8,128)(2,1)S(1)}, u32[]{:S(2)}, u32[]{:S(2)}) collective-permute-start(bf16[4,112,256]{2,1,0:T(8,128)(2,1)S(1)} %get-tuple-element.75), channel_id=1, source_target_pairs={{0,2},{1,3},{2,0},{3,1},{4,6},{5,7},{6,4},{7,5},{8,10},{9,11},{10,... | collective-permute-start | bytes 688136 | tf_op jit(solution)/shard_map/ppermute | solution.py:339
  105.9 5.4 %collective-permute-done.8 = bf16[4,112,256]{2,1,0:T(8,128)(2,1)S(1)} collective-permute-done((bf16[4,112,256]{2,1,0:T(8,128)(2,1)S(1)}, bf16[4,112,256]{2,1,0:T(8,128)(2,1)S(1)}, u32[]{:S(2)}, u32[]{:S(2)}) %collective-permute-start.8) | collective-permute-done | bytes 229408 | tf_op jit(solution)/shard_map/ppermute | solution.py:339
  111.3 5.3 %collective-permute-done.7 = bf16[4,112,384]{2,1,0:T(8,128)(2,1)S(1)} collective-permute-done((bf16[4,112,384]{2,1,0:T(8,128)(2,1)S(1)}, bf16[4,112,384]{2,1,0:T(8,128)(2,1)S(1)}, u32[]{:S(2)}, u32[]{:S(2)}) %collective-permute-start.7) | collective-permute-done | bytes 344096 | tf_op jit(solution)/shard_map/ppermute | solution.py:339
  118.9 4.0 %collective-permute-done.11 = bf16[2,112,256]{2,1,0:T(8,128)(2,1)S(1)} collective-permute-done((bf16[2,112,256]{2,1,0:T(8,128)(2,1)S(1)}, bf16[2,112,256]{2,1,0:T(8,128)(2,1)S(1)}, u32[]{:S(2)}, u32[]{:S(2)}) %collective-permute-start.11) | collective-permute-done | bytes 114720 | tf_op jit(solution)/shard_map/ppermute | solution.py:339
  123.0 1.6 %collective-permute-start.13 = (bf16[1,112,384]{2,1,0:T(8,128)(2,1)S(1)}, bf16[1,112,384]{2,1,0:T(8,128)(2,1)S(1)}, u32[]{:S(2)}, u32[]{:S(2)}) collective-permute-start(bf16[1,112,384]{2,1,0:T(8,128)(2,1)S(1)} %add_convert_fusion.22), channel_id=1, source_target_pairs={{0,16},{1,17},{2,18},{3,19},{4,20},{5,21},{6,22},{7,23},{8,24},{9,... | collective-permute-start | bytes 258056 | tf_op jit(solution)/shard_map/ppermute | solution.py:339
  124.5 1.5 %collective-permute-start.12 = (bf16[1,112,384]{2,1,0:T(8,128)(2,1)S(1)}, bf16[1,112,384]{2,1,0:T(8,128)(2,1)S(1)}, u32[]{:S(2)}, u32[]{:S(2)}) collective-permute-start(bf16[1,112,384]{2,1,0:T(8,128)(2,1)S(1)} %add_convert_fusion.23), channel_id=1, source_target_pairs={{0,16},{1,17},{2,18},{3,19},{4,20},{5,21},{6,22},{7,23},{8,24},{9,... | collective-permute-start | bytes 258056 | tf_op jit(solution)/shard_map/ppermute | solution.py:339
  126.1 1.6 %collective-permute-start.14 = (bf16[1,112,256]{2,1,0:T(8,128)(2,1)S(1)}, bf16[1,112,256]{2,1,0:T(8,128)(2,1)S(1)}, u32[]{:S(2)}, u32[]{:S(2)}) collective-permute-start(bf16[1,112,256]{2,1,0:T(8,128)(2,1)S(1)} %add_convert_fusion.25), channel_id=1, source_target_pairs={{0,16},{1,17},{2,18},{3,19},{4,20},{5,21},{6,22},{7,23},{8,24},{9,... | collective-permute-start | bytes 172040 | tf_op jit(solution)/shard_map/ppermute | solution.py:339
  128.6 4.0 %unpack.1 = f32[16,4,8192]{2,1,0:T(4,128)} custom-call(bf16[32,64,256]{2,1,0:T(8,128)(2,1)} %copy-done.1), custom_call_target="tpu_custom_call" | custom-call | tf_op jit(solution)/shard_map/unpack/pallas_call | solution.py:116
  (74 shorter events, 15.8 us)
Async XLA Ops:
  0.6 10.6 %copy-start.8 = (f32[3456]{0:T(1024)S(1)}, f32[3456]{0:T(1024)}, u32[]{:S(2)}) copy-start(f32[3456]{0:T(1024)} %param.23) | copy-start | bytes 41476
  3.8 11.6 %copy-start = (bf16[2,3456,256]{2,1,0:T(8,128)(2,1)S(1)}, bf16[2,3456,256]{2,1,0:T(8,128)(2,1)}, u32[]{:S(2)}) copy-start(bf16[2,3456,256]{2,1,0:T(8,128)(2,1)} %ci_hbm.1) | copy-start | bytes 10616836
  3.8 35.0 %all-to-all-start = ((bf16[32,136,128]{2,1,0:T(8,128)(2,1)}), bf16[32,136,128]{2,1,0:T(8,128)(2,1)}, u32[]{:S(2)}, u32[]{:S(2)}) async-start(bf16[32,136,128]{2,1,0:T(8,128)(2,1)} %pack.1), calls=%async_computation | async-start | bytes 2228224 | tf_op jit(solution)/shard_map/all_to_all | solution.py:390
  19.1 5.8 %copy-start.6 = (bf16[16,16,128]{2,1,0:T(8,128)(2,1)S(1)}, bf16[16,16,128]{2,1,0:T(8,128)(2,1)}, u32[]{:S(2)}) copy-start(bf16[16,16,128]{2,1,0:T(8,128)(2,1)} %p2.1) | copy-start | bytes 196612
  19.1 6.8 %copy-start.2 = (bf16[6,256,128]{2,1,0:T(8,128)(2,1)S(1)}, bf16[6,256,128]{2,1,0:T(8,128)(2,1)}, u32[]{:S(2)}) copy-start(bf16[6,256,128]{2,1,0:T(8,128)(2,1)} %p0.1) | copy-start | bytes 1179652
  24.9 2.8 %copy-start.9 = (f32[256]{0:T(256)S(1)}, f32[256]{0:T(256)}, u32[]{:S(2)}) copy-start(f32[256]{0:T(256)} %param.16) | copy-start | bytes 3076
  68.9 3.3 %collective-permute-start.3 = (bf16[16,112,384]{2,1,0:T(8,128)(2,1)}, bf16[16,112,384]{2,1,0:T(8,128)(2,1)S(1)}, u32[]{:S(2)}, u32[]{:S(2)}) collective-permute-start(bf16[16,112,384]{2,1,0:T(8,128)(2,1)} %get-tuple-element.39), channel_id=1, source_target_pairs={{0,1},{1,0},{2,3},{3,2},{4,5},{5,4},{6,7},{7,6},{8,9},{9,8},{10,11... | collective-permute-start | bytes 4128776 | tf_op jit(solution)/shard_map/ppermute | solution.py:339
  68.9 7.5 %collective-permute-start.1 = (bf16[16,112,384]{2,1,0:T(8,128)(2,1)}, bf16[16,112,384]{2,1,0:T(8,128)(2,1)S(1)}, u32[]{:S(2)}, u32[]{:S(2)}) collective-permute-start(bf16[16,112,384]{2,1,0:T(8,128)(2,1)} %get-tuple-element.37), channel_id=1, source_target_pairs={{0,1},{1,0},{2,3},{3,2},{4,5},{5,4},{6,7},{7,6},{8,9},{9,8},{10,11... | collective-permute-start | bytes 4128776 | tf_op jit(solution)/shard_map/ppermute | solution.py:339
  69.4 9.7 %collective-permute-start = (bf16[16,112,256]{2,1,0:T(8,128)(2,1)}, bf16[16,112,256]{2,1,0:T(8,128)(2,1)S(1)}, u32[]{:S(2)}, u32[]{:S(2)}) collective-permute-start(bf16[16,112,256]{2,1,0:T(8,128)(2,1)} %get-tuple-element.35), channel_id=1, source_target_pairs={{0,1},{1,0},{2,3},{3,2},{4,5},{5,4},{6,7},{7,6},{8,9},{9,8},{10,11... | collective-permute-start | bytes 2752520 | tf_op jit(solution)/shard_map/ppermute | solution.py:339
  72.3 4.1 %copy-start.3 = (bf16[16,112,384]{2,1,0:T(8,128)(2,1)S(1)}, bf16[16,112,384]{2,1,0:T(8,128)(2,1)}, u32[]{:S(2)}) copy-start(bf16[16,112,384]{2,1,0:T(8,128)(2,1)} %get-tuple-element.36) | copy-start | bytes 4128772
  74.9 25.8 %collective-permute-start.4 = (bf16[8,112,384]{2,1,0:T(8,128)(2,1)}, bf16[8,112,384]{2,1,0:T(8,128)(2,1)}, u32[]{:S(2)}, u32[]{:S(2)}) collective-permute-start(bf16[8,112,384]{2,1,0:T(8,128)(2,1)} %get-tuple-element.65), channel_id=1, source_target_pairs={{0,4},{1,5},{2,6},{3,7},{4,0},{5,1},{6,2},{7,3},{8,12},{9,13},{10,... | collective-permute-start | bytes 2064392 | tf_op jit(solution)/shard_map/ppermute | solution.py:339
  77.6 23.0 %collective-permute-start.2 = (bf16[8,112,384]{2,1,0:T(8,128)(2,1)}, bf16[8,112,384]{2,1,0:T(8,128)(2,1)}, u32[]{:S(2)}, u32[]{:S(2)}) collective-permute-start(bf16[8,112,384]{2,1,0:T(8,128)(2,1)} %get-tuple-element.66), channel_id=1, source_target_pairs={{0,2},{1,3},{2,0},{3,1},{4,6},{5,7},{6,4},{7,5},{8,10},{9,11},{10,... | collective-permute-start | bytes 2064392 | tf_op jit(solution)/shard_map/ppermute | solution.py:339
  80.1 20.5 %collective-permute-start.5 = (bf16[8,112,256]{2,1,0:T(8,128)(2,1)}, bf16[8,112,256]{2,1,0:T(8,128)(2,1)S(1)}, u32[]{:S(2)}, u32[]{:S(2)}) collective-permute-start(bf16[8,112,256]{2,1,0:T(8,128)(2,1)} %get-tuple-element.69), channel_id=1, source_target_pairs={{0,8},{1,9},{2,10},{3,11},{4,12},{5,13},{6,14},{7,15},{8,0},{9,1},... | collective-permute-start | bytes 1376264 | tf_op jit(solution)/shard_map/ppermute | solution.py:339
  80.1 47.5 %all-to-all-start.1 = ((bf16[32,64,256]{2,1,0:T(8,128)(2,1)}), bf16[32,64,256]{2,1,0:T(8,128)(2,1)S(1)}, u32[]{:S(2)}, u32[]{:S(2)}) async-start(bf16[32,64,256]{2,1,0:T(8,128)(2,1)} %bitcast.34), calls=%async_computation.1 | async-start | bytes 2097152 | tf_op jit(solution)/shard_map/all_to_all | solution.py:444
  101.9 14.6 %collective-permute-start.7 = (bf16[4,112,384]{2,1,0:T(8,128)(2,1)S(1)}, bf16[4,112,384]{2,1,0:T(8,128)(2,1)S(1)}, u32[]{:S(2)}, u32[]{:S(2)}) collective-permute-start(bf16[4,112,384]{2,1,0:T(8,128)(2,1)S(1)} %get-tuple-element.71), channel_id=1, source_target_pairs={{0,8},{1,9},{2,10},{3,11},{4,12},{5,13},{6,14},{7,15},{8,0},{9,1},... | collective-permute-start | bytes 1032200 | tf_op jit(solution)/shard_map/ppermute | solution.py:339
  103.6 13.0 %collective-permute-start.6 = (bf16[4,112,384]{2,1,0:T(8,128)(2,1)S(1)}, bf16[4,112,384]{2,1,0:T(8,128)(2,1)S(1)}, u32[]{:S(2)}, u32[]{:S(2)}) collective-permute-start(bf16[4,112,384]{2,1,0:T(8,128)(2,1)S(1)} %get-tuple-element.72), channel_id=1, source_target_pairs={{0,4},{1,5},{2,6},{3,7},{4,0},{5,1},{6,2},{7,3},{8,12},{9,13},{10,... | collective-permute-start | bytes 1032200 | tf_op jit(solution)/shard_map/ppermute | solution.py:339
  104.1 7.2 %collective-permute-start.8 = (bf16[4,112,256]{2,1,0:T(8,128)(2,1)S(1)}, bf16[4,112,256]{2,1,0:T(8,128)(2,1)S(1)}, u32[]{:S(2)}, u32[]{:S(2)}) collective-permute-start(bf16[4,112,256]{2,1,0:T(8,128)(2,1)S(1)} %get-tuple-element.75), channel_id=1, source_target_pairs={{0,2},{1,3},{2,0},{3,1},{4,6},{5,7},{6,4},{7,5},{8,10},{9,11},{10,... | collective-permute-start | bytes 688136 | tf_op jit(solution)/shard_map/ppermute | solution.py:339
  116.7 6.3 %collective-permute-start.10 = (bf16[2,112,384]{2,1,0:T(8,128)(2,1)S(1)}, bf16[2,112,384]{2,1,0:T(8,128)(2,1)S(1)}, u32[]{:S(2)}, u32[]{:S(2)}) collective-permute-start(bf16[2,112,384]{2,1,0:T(8,128)(2,1)S(1)} %get-tuple-element.77), channel_id=1, source_target_pairs={{0,2},{1,3},{2,0},{3,1},{4,6},{5,7},{6,4},{7,5},{8,10},{9,11},{10,... | collective-permute-start | bytes 516104 | tf_op jit(solution)/shard_map/ppermute | solution.py:339
  117.4 5.6 %collective-permute-start.9 = (bf16[2,112,384]{2,1,0:T(8,128)(2,1)S(1)}, bf16[2,112,384]{2,1,0:T(8,128)(2,1)S(1)}, u32[]{:S(2)}, u32[]{:S(2)}) collective-permute-start(bf16[2,112,384]{2,1,0:T(8,128)(2,1)S(1)} %get-tuple-element.78), channel_id=1, source_target_pairs={{0,8},{1,9},{2,10},{3,11},{4,12},{5,13},{6,14},{7,15},{8,0},{9,1},... | collective-permute-start | bytes 516104 | tf_op jit(solution)/shard_map/ppermute | solution.py:339
  118.1 4.9 %collective-permute-start.11 = (bf16[2,112,256]{2,1,0:T(8,128)(2,1)S(1)}, bf16[2,112,256]{2,1,0:T(8,128)(2,1)S(1)}, u32[]{:S(2)}, u32[]{:S(2)}) collective-permute-start(bf16[2,112,256]{2,1,0:T(8,128)(2,1)S(1)} %get-tuple-element.81), channel_id=1, source_target_pairs={{0,4},{1,5},{2,6},{3,7},{4,0},{5,1},{6,2},{7,3},{8,12},{9,13},{10,... | collective-permute-start | bytes 344072 | tf_op jit(solution)/shard_map/ppermute | solution.py:339
  122.9 9.7 %copy-start.7 = (bf16[2,112,256]{2,1,0:T(8,128)(2,1)}, bf16[2,112,256]{2,1,0:T(8,128)(2,1)S(1)}, u32[]{:S(2)}) copy-start(bf16[2,112,256]{2,1,0:T(8,128)(2,1)S(1)} %collective-permute-done.11) | copy-start | bytes 344068
  123.0 10.9 %collective-permute-start.13 = (bf16[1,112,384]{2,1,0:T(8,128)(2,1)S(1)}, bf16[1,112,384]{2,1,0:T(8,128)(2,1)S(1)}, u32[]{:S(2)}, u32[]{:S(2)}) collective-permute-start(bf16[1,112,384]{2,1,0:T(8,128)(2,1)S(1)} %add_convert_fusion.22), channel_id=1, source_target_pairs={{0,16},{1,17},{2,18},{3,19},{4,20},{5,21},{6,22},{7,23},{8,24},{9,... | collective-permute-start | bytes 258056 | tf_op jit(solution)/shard_map/ppermute | solution.py:339
  124.5 9.3 %collective-permute-start.12 = (bf16[1,112,384]{2,1,0:T(8,128)(2,1)S(1)}, bf16[1,112,384]{2,1,0:T(8,128)(2,1)S(1)}, u32[]{:S(2)}, u32[]{:S(2)}) collective-permute-start(bf16[1,112,384]{2,1,0:T(8,128)(2,1)S(1)} %add_convert_fusion.23), channel_id=1, source_target_pairs={{0,16},{1,17},{2,18},{3,19},{4,20},{5,21},{6,22},{7,23},{8,24},{9,... | collective-permute-start | bytes 258056 | tf_op jit(solution)/shard_map/ppermute | solution.py:339
  126.1 7.8 %collective-permute-start.14 = (bf16[1,112,256]{2,1,0:T(8,128)(2,1)S(1)}, bf16[1,112,256]{2,1,0:T(8,128)(2,1)S(1)}, u32[]{:S(2)}, u32[]{:S(2)}) collective-permute-start(bf16[1,112,256]{2,1,0:T(8,128)(2,1)S(1)} %add_convert_fusion.25), channel_id=1, source_target_pairs={{0,16},{1,17},{2,18},{3,19},{4,20},{5,21},{6,22},{7,23},{8,24},{9,... | collective-permute-start | bytes 172040 | tf_op jit(solution)/shard_map/ppermute | solution.py:339
  (5 other events, 10.8 us)

commit v3 on v2

--- a/solution.py
+++ b/solution.py
@@ -130,7 +130,7 @@
         x_ref,
         dense_ref,
         row_ref,
-        col_ref,
+        col_hbm,
         pt0,
         pt1,
         pt2,
@@ -158,6 +158,7 @@
         low,
         gate0,
         gate1,
+        col_ref,
         sems,
         out_sems,
     ):
@@ -171,11 +172,13 @@
         uses = [("cit", 0), ("cot", 0), ("cit", 1), ("cot", 1), ("co", 1), ("ci", 1), ("co", 0), ("ci", 0)]
 
         def fetch(n):
+            if n == len(uses):
+                return pltpu.make_async_copy(col_hbm, col_ref, sems.at[n])
             name, layer = uses[n]
             source, target = names[name]
             return pltpu.make_async_copy(source.at[layer], target.at[layer], sems.at[n])
 
-        for n in range(len(uses)):
+        for n in (0, len(uses), *range(1, len(uses))):
             fetch(n).start()
         written = ((start, start_hbm), (layer1, layer1_hbm), (low1, low1_hbm), (low0, low0_hbm))
 
@@ -211,6 +214,7 @@
         fetch(0).wait()
         hidden0 = dot(cit_ref[0], start[...]).astype(BF)
         small[0] = hidden0
+        fetch(len(uses)).wait()
         fetch(1).wait()
 
         def fwd0(i):
@@ -286,34 +290,38 @@
     return kernel
 
 
-def make_grads(orders, splits, devices, chunk, chunk_pad):
+def make_grads(pieces, biases, orders, cols, devices, chunk, chunk_pad):
     half = devices // 2
-    colors = len(splits)
-
-    def kernel(me_ref, start, layer1, low1, low0, small, *refs):
-        los, his, acc = refs[:colors], refs[colors : 2 * colors], refs[2 * colors]
-        group, rows = start.shape
-        rank = small.shape[1]
+    colors = len(pieces)
+
+    def kernel(me_ref, small, *refs):
+        wides, (los, his, acc) = refs[: -2 * colors - 1], (
+            refs[-2 * colors - 1 : -colors - 1],
+            refs[-colors - 1 : -1],
+            refs[-1],
+        )
+        group, rows = wides[0].shape
         subs = group // chunk
         me = me_ref[0]
-        acc[:, 0:rank] = dot(low1[...], small[1], NT)
-        acc[:, rank : 2 * rank] = dot(layer1[...], small[2], NT)
-        acc[:, 2 * rank : 3 * rank] = dot(low0[...], small[0], NT)
-        acc[:, 3 * rank : 4 * rank] = dot(start[...], small[3], NT)
+        spare = chunk_pad - chunk
+        at = 0
+        for parts in pieces:
+            for wide, low, first, last in parts:
+                acc[:, at : at + last - first] = dot(wides[wide][...], small[low, first:last, :], NT)
+                at += last - first
         ones = jnp.ones((8, rows), BF)
-        biases = (dot(ones, low1[...], NT), dot(ones, low0[...], NT))
-        spare = chunk_pad - chunk
+        sums = [None if w is None else dot(ones, wides[w][...], NT) for w in biases]
         for s in range(subs):
             d = pl.program_id(0) * subs + s
             at = 0
-            for which, cols in enumerate(splits):
-                piece = acc[s * chunk : (s + 1) * chunk, at : at + cols]
-                at += cols
-                if which < 2:
-                    tail = biases[which][0:spare, s * chunk : (s + 1) * chunk]
-                    tail = jnp.concatenate([tail, jnp.zeros((spare, cols - chunk), F32)], 1)
+            for which in range(colors):
+                piece = acc[s * chunk : (s + 1) * chunk, at : at + cols[which]]
+                at += cols[which]
+                if sums[which] is not None:
+                    tail = sums[which][0:spare, s * chunk : (s + 1) * chunk]
+                    tail = jnp.concatenate([tail, jnp.zeros((spare, cols[which] - chunk), F32)], 1)
                 else:
-                    tail = jnp.zeros((spare, cols), F32)
+                    tail = jnp.zeros((spare, cols[which]), F32)
                 value = jnp.concatenate([piece, tail], 0).astype(BF)
                 place = position_of(d ^ me, orders[which])
 
@@ -326,6 +334,33 @@
                     his[which][place - half] = value
 
     return kernel
+
+
+def weight_grads(me, small, wides, pieces, biases, orders, devices, chunk, chunk_pad):
+    width, rows = wides[0].shape
+    group = chunk
+    while group % 16:
+        group += chunk
+    if width % (2 * group) == 0:
+        group *= 2
+    colors = len(pieces)
+    cols = [sum(last - first for _, _, first, last in p) for p in pieces]
+    part = pl.BlockSpec((group, rows), lambda i: (i, 0))
+    half = [jax.ShapeDtypeStruct((devices // 2, chunk_pad, c), BF) for c in cols]
+    outs = pl.pallas_call(
+        make_grads(pieces, biases, orders, cols, devices, chunk, chunk_pad),
+        grid=(width // group,),
+        in_specs=[pl.BlockSpec(memory_space=pltpu.SMEM), pl.BlockSpec(small.shape, lambda i: (0, 0, 0))]
+        + [part] * len(wides),
+        out_specs=[pl.BlockSpec(h.shape, lambda i: (0, 0, 0)) for h in half + half],
+        out_shape=half + half,
+        scratch_shapes=[pltpu.VMEM((group, sum(cols)), F32)],
+        compiler_params=pltpu.CompilerParams(vmem_limit_bytes=46 << 20),
+        cost_estimate=pl.CostEstimate(
+            flops=2 * width * sum(cols) * rows, bytes_accessed=4 * width * sum(cols), transcendentals=0
+        ),
+    )(me, small, *wides)
+    return list(outs[:colors]), list(outs[colors:])
 
 
 def add_pair(a, b):
@@ -398,7 +433,7 @@
     wide = jax.ShapeDtypeStruct((width, rows), BF)
     back, start, layer1, low1, low0, small = pl.pallas_call(
         make_step(tables, devices, blocks_here),
-        in_specs=[smem] + [vmem] * 10 + [hbm] * 4,
+        in_specs=[smem] + [vmem] * 3 + [hbm] + [vmem] * 6 + [hbm] * 4,
         out_specs=[vmem] + [hbm] * 4 + [vmem],
         out_shape=[
             jax.ShapeDtypeStruct((blocks_here * devices, BLOCK_WIDTH, rows), BF),
@@ -417,7 +452,8 @@
             pltpu.VMEM((width, rows), BF),
             pltpu.VMEM((width, rows), F32),
             pltpu.VMEM((width, rows), F32),
-            pltpu.SemaphoreType.DMA((8,)),
+            pltpu.VMEM((width, 3), F32),
+            pltpu.SemaphoreType.DMA((9,)),
             pltpu.SemaphoreType.DMA((4,)),
         ],
         compiler_params=pltpu.CompilerParams(vmem_limit_bytes=60 << 20),
@@ -443,32 +479,20 @@
     back = back.reshape(devices, blocks_here * BLOCK_WIDTH, rows)
     back = lax.all_to_all(back, AXES, 0, 0, tiled=True)
 
-    group = chunk
-    while group % 16:
-        group += chunk
-    if width % (2 * group) == 0:
-        group *= 2
-    part = pl.BlockSpec((group, rows), lambda i: (i, 0))
-    half = [jax.ShapeDtypeStruct((devices // 2, chunk_pad, c), BF) for c in splits]
-    outs = pl.pallas_call(
-        make_grads(orders, splits, devices, chunk, chunk_pad),
-        grid=(width // group,),
-        in_specs=[smem, part, part, part, part, pl.BlockSpec((4, rank, rows), lambda i: (0, 0, 0))],
-        out_specs=[pl.BlockSpec(h.shape, lambda i: (0, 0, 0)) for h in half + half],
-        out_shape=half + half,
-        scratch_shapes=[pltpu.VMEM((group, 4 * rank), F32)],
-        compiler_params=pltpu.CompilerParams(vmem_limit_bytes=60 << 20),
-        cost_estimate=pl.CostEstimate(flops=8 * width * rank * rows, bytes_accessed=16 << 20, transcendentals=0),
-        name="grads",
-    )(me, start, layer1, low1, low0, small)
-    los, his = list(outs[:colors]), list(outs[colors:])
+    cut = splits[0] - rank
+    fixed = (devices, chunk, chunk_pad)
+    los, his = weight_grads(
+        me, small, (low1, layer1, low0, start),
+        [[(0, 1, 0, rank), (1, 2, 0, cut)], [(1, 2, cut, rank), (2, 0, 0, rank)], [(3, 3, 0, rank)]],
+        [0, 2, None], orders, *fixed,
+    )
     sums = reduce_pieces(los, his, orders, devices)
     pooled_grad = unpack(back)
     bias1, bias0 = sums[0][chunk, :chunk], sums[1][chunk, :chunk]
-    flat = jnp.concatenate([x[:chunk] for x in sums], 1)
+    flat = jnp.concatenate([x[:chunk] for x in sums], 1).astype(F32)
     out1, in1, out0, in0 = [flat[:, i * rank : (i + 1) * rank] for i in range(4)]
-    grad_in = jnp.stack([in0, in1]).astype(F32)
-    grad_out = jnp.stack([out0.T, out1.T]).astype(F32)
+    grad_in = jnp.transpose(jnp.stack([in0, in1], 1), (1, 0, 2))
+    grad_out = jnp.transpose(jnp.stack([out0, out1], 1), (1, 2, 0))
     grad_bias = jnp.stack([bias0, bias1]).astype(F32)
     return (pooled_grad, grad_in, grad_out, grad_bias)
 

time: 137 us -> 133 us (0.971)
  Pallas kernels: 37.2 us -> 33.6 us
  other arithmetic: 9.77 us -> 8.29 us
    pallas_call x1, Pallas kernels: 13.1 us -> 10.1 us  [weight_grads(): pl.pallas_call(make_grads(pieces, biases, orders, cols, devices, chunk, c...]
    convert_element_type x14 -> x13, other arithmetic: 7.89 us -> 6.37 us  [add_pair(): return (a.astype(F32) + b.astype(F32)).astype(BF)]
    unnamed x29 -> x25, local copies, waits for them, and re-layouts: 15 us -> 16 us
where the time goes in v3:
time: 133 us; the launch traced here: 132 us
  waiting for transfers between devices  46.7 us (35%)
  Pallas kernels  33.6 us (25%)
  starting transfers between devices  23.3 us (18%)
  local copies, waits for them, and re-layouts  19.5 us (15%)
  other arithmetic  8.29 us (6%)
    ppermute x15, waiting for transfers between devices, reduce_pieces(): lax.ppermute(h, AXES, [(i, i ^ o[k]) for i in range(devices)])  36.1 us
    pallas_call x1, Pallas kernels, run(): pl.pallas_call(make_step(tables, devices, blocks_here), in_specs=[smem] +...  16.4 us
    unnamed x25, local copies, waits for them, and re-layouts  16 us
    ppermute x15, starting transfers between devices, reduce_pieces(): lax.ppermute(h, AXES, [(i, i ^ o[k]) for i in range(devices)])  13 us
    all_to_all x1, waiting for transfers between devices, run(): lax.all_to_all(pack(pooled, sample_weight, devices), AXES, 0, 0, tiled=True)  10.7 us
    pallas_call x1, Pallas kernels, weight_grads(): pl.pallas_call(make_grads(pieces, biases, orders, cols, devices, chunk, c...  10.1 us
    all_to_all x1, starting transfers between devices, run(): lax.all_to_all(pack(pooled, sample_weight, devices), AXES, 0, 0, tiled=True)  7.44 us
    convert_element_type x13, other arithmetic, add_pair(): return (a.astype(F32) + b.astype(F32)).astype(BF)  6.37 us
  transfers between devices with their start and end apart: 17, of which 7 were waited for; matrix products, arithmetic and copies ran while one was open for 18% of the time, Pallas kernels for 3%

profile of v3, /device:TPU:0, one launch (start us, length us, event | category | flops | bytes accessed | tf_op | source)
XLA Modules:
  0.0 132.3 jit_solution(9250060707628980039)
XLA Ops:
  0.6 3.2 %pack.1 = bf16[32,136,128]{2,1,0:T(8,128)(2,1)} custom-call(f32[2,128]{1,0:T(2,128)} %bitcast.42, bf16[16,4,8192]{2,1,0:T(4,128)(2,1)} %x_ref.1), custom_call_target="tpu_custom_call" | custom-call | tf_op jit(solution)/shard_map/pack/pallas_call | solution.py:85
  3.8 7.4 %all-to-all-start = ((bf16[32,136,128]{2,1,0:T(8,128)(2,1)}), bf16[32,136,128]{2,1,0:T(8,128)(2,1)}, u32[]{:S(2)}, u32[]{:S(2)}) async-start(bf16[32,136,128]{2,1,0:T(8,128)(2,1)} %pack.1), calls=%async_computation | async-start | bytes 2228224 | tf_op jit(solution)/shard_map/all_to_all | solution.py:425
  12.8 2.6 %copy.38.col_hbm = f32[3456,3]{1,0:T(8,128)} copy(f32[3456,3]{0,1:T(4,128)} %pad_maximum_fusion) | data formatting | bytes 82944 | tf_op jit(solution)/shard_map/stack | solution.py:427
  15.4 3.7 %copy.36 = bf16[2,3456,256]{1,2,0:T(8,128)(2,1)} copy(bf16[2,3456,256]{2,1,0:T(8,128)(2,1)S(1)} %copy-done.1) | data formatting | bytes 7077888 | tf_op args[8]
  19.1 5.8 %copy.37 = bf16[2,256,3456]{1,2,0:T(8,128)(2,1)} copy(bf16[2,256,3456]{2,1,0:T(8,128)(2,1)} %co_hbm.1) | data formatting | bytes 7077888 | tf_op args[9]
  28.2 10.7 %all-to-all-done.x_ref = bf16[32,136,128]{2,1,0:T(8,128)(2,1)} async-done(((bf16[32,136,128]{2,1,0:T(8,128)(2,1)}), bf16[32,136,128]{2,1,0:T(8,128)(2,1)}, u32[]{:S(2)}, u32[]{:S(2)}) %all-to-all-start) | async-done | bytes 1114144 | tf_op jit(solution)/shard_map/all_to_all | solution.py:425
  38.9 16.4 %step.1 = (bf16[128,16,256]{2,1,0:T(8,128)(2,1)}, bf16[3456,256]{1,0:T(8,128)(2,1)}, bf16[3456,256]{1,0:T(8,128)(2,1)}, bf16[3456,256]{1,0:T(8,128)(2,1)}, bf16[...) custom-call(s32[128]{0:T(128)} %slot_ref.1, bf16[32,136,128]{2,1,0:T(8,128)(2,1)} %all-to-all-done.x_ref, ...), custom_call_target="tpu_custom_call" | custom-call | flops 3623878656 | bytes 20971520 | tf_op jit(solution)/shard_map/step/pallas_call | solution.py:434
  56.3 10.1 %shard_map.147 = (bf16[16,112,384]{2,1,0:T(8,128)(2,1)S(1)}, bf16[16,112,384]{2,1,0:T(8,128)(2,1)S(1)}, bf16[16,112,256]{2,1,0:T(8,128)(2,1)S(1)}, bf16[16,112,3...) custom-call(s32[1]{0:T(128)} %bitcast.11.me_ref, ...), custom_call_target="tpu_custom_call" | custom-call | flops 1811939328 | bytes 14155776 | tf_op jit(solution)/shard_map/pallas_call | solution.py:350
  67.1 2.5 %collective-permute-done.2 = bf16[16,112,384]{2,1,0:T(8,128)(2,1)S(1)} collective-permute-done((bf16[16,112,384]{2,1,0:T(8,128)(2,1)S(1)}, bf16[16,112,384]{2,1,0:T(8,128)(2,1)S(1)}, u32[]{:S(2)}, u32[]{:S(2)}) %collective-permute-start.2) | collective-permute-done | bytes 1376288 | tf_op jit(solution)/shard_map/ppermute | solution.py:374
  70.8 1.5 %collective-permute-start.3 = (bf16[8,112,384]{2,1,0:T(8,128)(2,1)}, bf16[8,112,384]{2,1,0:T(8,128)(2,1)}, u32[]{:S(2)}, u32[]{:S(2)}) collective-permute-start(bf16[8,112,384]{2,1,0:T(8,128)(2,1)} %get-tuple-element.65), channel_id=1, source_target_pairs={{0,4},{1,5},{2,6},{3,7},{4,0},{5,1},{6,2},{7,3},{8,12},{9,13},{10,... | collective-permute-start | bytes 2064392 | tf_op jit(solution)/shard_map/ppermute | solution.py:374
  73.5 1.5 %collective-permute-start.1 = (bf16[8,112,384]{2,1,0:T(8,128)(2,1)}, bf16[8,112,384]{2,1,0:T(8,128)(2,1)}, u32[]{:S(2)}, u32[]{:S(2)}) collective-permute-start(bf16[8,112,384]{2,1,0:T(8,128)(2,1)} %get-tuple-element.66), channel_id=1, source_target_pairs={{0,2},{1,3},{2,0},{3,1},{4,6},{5,7},{6,4},{7,5},{8,10},{9,11},{10,... | collective-permute-start | bytes 2064392 | tf_op jit(solution)/shard_map/ppermute | solution.py:374
  76.0 2.9 %all-to-all-start.1 = ((bf16[32,64,256]{2,1,0:T(8,128)(2,1)}), bf16[32,64,256]{2,1,0:T(8,128)(2,1)S(1)}, u32[]{:S(2)}, u32[]{:S(2)}) async-start(bf16[32,64,256]{2,1,0:T(8,128)(2,1)} %bitcast.38), calls=%async_computation.1 | async-start | bytes 2097152 | tf_op jit(solution)/shard_map/all_to_all | solution.py:480
  78.9 17.7 %collective-permute-done.5 = bf16[8,112,256]{2,1,0:T(8,128)(2,1)S(1)} collective-permute-done((bf16[8,112,256]{2,1,0:T(8,128)(2,1)}, bf16[8,112,256]{2,1,0:T(8,128)(2,1)S(1)}, u32[]{:S(2)}, u32[]{:S(2)}) %collective-permute-start.5) | collective-permute-done | bytes 458784 | tf_op jit(solution)/shard_map/ppermute | solution.py:374
  96.6 1.3 add_convert_fusion.6
  98.2 1.3 add_convert_fusion.8
  100.0 1.7 %collective-permute-start.8 = (bf16[4,112,256]{2,1,0:T(8,128)(2,1)S(1)}, bf16[4,112,256]{2,1,0:T(8,128)(2,1)S(1)}, u32[]{:S(2)}, u32[]{:S(2)}) collective-permute-start(bf16[4,112,256]{2,1,0:T(8,128)(2,1)S(1)} %get-tuple-element.75), channel_id=1, source_target_pairs={{0,2},{1,3},{2,0},{3,1},{4,6},{5,7},{6,4},{7,5},{8,10},{9,11},{10,... | collective-permute-start | bytes 688136 | tf_op jit(solution)/shard_map/ppermute | solution.py:374
  101.7 5.4 %collective-permute-done.8 = bf16[4,112,256]{2,1,0:T(8,128)(2,1)S(1)} collective-permute-done((bf16[4,112,256]{2,1,0:T(8,128)(2,1)S(1)}, bf16[4,112,256]{2,1,0:T(8,128)(2,1)S(1)}, u32[]{:S(2)}, u32[]{:S(2)}) %collective-permute-start.8) | collective-permute-done | bytes 229408 | tf_op jit(solution)/shard_map/ppermute | solution.py:374
  107.2 5.3 %collective-permute-done.7 = bf16[4,112,384]{2,1,0:T(8,128)(2,1)S(1)} collective-permute-done((bf16[4,112,384]{2,1,0:T(8,128)(2,1)S(1)}, bf16[4,112,384]{2,1,0:T(8,128)(2,1)S(1)}, u32[]{:S(2)}, u32[]{:S(2)}) %collective-permute-start.7) | collective-permute-done | bytes 344096 | tf_op jit(solution)/shard_map/ppermute | solution.py:374
  115.0 3.8 %collective-permute-done.11 = bf16[2,112,256]{2,1,0:T(8,128)(2,1)S(1)} collective-permute-done((bf16[2,112,256]{2,1,0:T(8,128)(2,1)S(1)}, bf16[2,112,256]{2,1,0:T(8,128)(2,1)S(1)}, u32[]{:S(2)}, u32[]{:S(2)}) %collective-permute-start.11) | collective-permute-done | bytes 114720 | tf_op jit(solution)/shard_map/ppermute | solution.py:374
  118.8 1.5 %collective-permute-start.13 = (bf16[1,112,384]{2,1,0:T(8,128)(2,1)S(1)}, bf16[1,112,384]{2,1,0:T(8,128)(2,1)S(1)}, u32[]{:S(2)}, u32[]{:S(2)}) collective-permute-start(bf16[1,112,384]{2,1,0:T(8,128)(2,1)S(1)} %add_convert_fusion.21), channel_id=1, source_target_pairs={{0,16},{1,17},{2,18},{3,19},{4,20},{5,21},{6,22},{7,23},{8,24},{9,... | collective-permute-start | bytes 258056 | tf_op jit(solution)/shard_map/ppermute | solution.py:374
  120.4 1.5 %collective-permute-start.12 = (bf16[1,112,384]{2,1,0:T(8,128)(2,1)S(1)}, bf16[1,112,384]{2,1,0:T(8,128)(2,1)S(1)}, u32[]{:S(2)}, u32[]{:S(2)}) collective-permute-start(bf16[1,112,384]{2,1,0:T(8,128)(2,1)S(1)} %add_convert_fusion.22), channel_id=1, source_target_pairs={{0,16},{1,17},{2,18},{3,19},{4,20},{5,21},{6,22},{7,23},{8,24},{9,... | collective-permute-start | bytes 258056 | tf_op jit(solution)/shard_map/ppermute | solution.py:374
  121.9 1.5 %collective-permute-start.14 = (bf16[1,112,256]{2,1,0:T(8,128)(2,1)S(1)}, bf16[1,112,256]{2,1,0:T(8,128)(2,1)S(1)}, u32[]{:S(2)}, u32[]{:S(2)}) collective-permute-start(bf16[1,112,256]{2,1,0:T(8,128)(2,1)S(1)} %add_convert_fusion.26), channel_id=1, source_target_pairs={{0,16},{1,17},{2,18},{3,19},{4,20},{5,21},{6,22},{7,23},{8,24},{9,... | collective-permute-start | bytes 172040 | tf_op jit(solution)/shard_map/ppermute | solution.py:374
  124.5 4.0 %unpack.1 = f32[16,4,8192]{2,1,0:T(4,128)} custom-call(bf16[32,64,256]{2,1,0:T(8,128)(2,1)} %copy-done.2), custom_call_target="tpu_custom_call" | custom-call | tf_op jit(solution)/shard_map/unpack/pallas_call | solution.py:116
  128.4 1.3 collective-permute-done.14
  (70 shorter events, 17.0 us)
Async XLA Ops:
  0.6 10.6 %copy-start.6 = (f32[3456]{0:T(1024)S(1)}, f32[3456]{0:T(1024)}, u32[]{:S(2)}) copy-start(f32[3456]{0:T(1024)} %param.23) | copy-start | bytes 41476
  3.8 11.6 %copy-start.1 = (bf16[2,3456,256]{2,1,0:T(8,128)(2,1)S(1)}, bf16[2,3456,256]{2,1,0:T(8,128)(2,1)}, u32[]{:S(2)}) copy-start(bf16[2,3456,256]{2,1,0:T(8,128)(2,1)} %ci_hbm.1) | copy-start | bytes 10616836
  3.8 35.0 %all-to-all-start = ((bf16[32,136,128]{2,1,0:T(8,128)(2,1)}), bf16[32,136,128]{2,1,0:T(8,128)(2,1)}, u32[]{:S(2)}, u32[]{:S(2)}) async-start(bf16[32,136,128]{2,1,0:T(8,128)(2,1)} %pack.1), calls=%async_computation | async-start | bytes 2228224 | tf_op jit(solution)/shard_map/all_to_all | solution.py:425
  19.1 5.8 %copy-start.5 = (bf16[16,16,128]{2,1,0:T(8,128)(2,1)S(1)}, bf16[16,16,128]{2,1,0:T(8,128)(2,1)}, u32[]{:S(2)}) copy-start(bf16[16,16,128]{2,1,0:T(8,128)(2,1)} %p2.1) | copy-start | bytes 196612
  19.1 6.8 %copy-start.3 = (bf16[6,256,128]{2,1,0:T(8,128)(2,1)S(1)}, bf16[6,256,128]{2,1,0:T(8,128)(2,1)}, u32[]{:S(2)}) copy-start(bf16[6,256,128]{2,1,0:T(8,128)(2,1)} %p0.1) | copy-start | bytes 1179652
  24.9 2.0 %copy-start.4 = (bf16[4,64,128]{2,1,0:T(8,128)(2,1)S(1)}, bf16[4,64,128]{2,1,0:T(8,128)(2,1)}, u32[]{:S(2)}) copy-start(bf16[4,64,128]{2,1,0:T(8,128)(2,1)} %p1.1) | copy-start | bytes 196612
  24.9 2.8 %copy-start.8 = (s32[256]{0:T(256)S(1)}, s32[256]{0:T(256)}, u32[]{:S(2)}) copy-start(s32[256]{0:T(256)} %param.15) | copy-start | bytes 3076
  24.9 2.8 %copy-start.7 = (f32[256]{0:T(256)S(1)}, f32[256]{0:T(256)}, u32[]{:S(2)}) copy-start(f32[256]{0:T(256)} %param.16) | copy-start | bytes 3076
  66.4 3.2 %collective-permute-start.2 = (bf16[16,112,384]{2,1,0:T(8,128)(2,1)S(1)}, bf16[16,112,384]{2,1,0:T(8,128)(2,1)S(1)}, u32[]{:S(2)}, u32[]{:S(2)}) collective-permute-start(bf16[16,112,384]{2,1,0:T(8,128)(2,1)S(1)} %get-tuple-element.37), channel_id=1, source_target_pairs={{0,1},{1,0},{2,3},{3,2},{4,5},{5,4},{6,7},{7,6},{8,9},{9,8},{10,11... | collective-permute-start | bytes 4128776 | tf_op jit(solution)/shard_map/ppermute | solution.py:374
  66.5 5.8 %collective-permute-start = (bf16[16,112,384]{2,1,0:T(8,128)(2,1)S(1)}, bf16[16,112,384]{2,1,0:T(8,128)(2,1)S(1)}, u32[]{:S(2)}, u32[]{:S(2)}) collective-permute-start(bf16[16,112,384]{2,1,0:T(8,128)(2,1)S(1)} %get-tuple-element.35), channel_id=1, source_target_pairs={{0,1},{1,0},{2,3},{3,2},{4,5},{5,4},{6,7},{7,6},{8,9},{9,8},{10,11... | collective-permute-start | bytes 4128776 | tf_op jit(solution)/shard_map/ppermute | solution.py:374
  67.0 8.0 %collective-permute-start.4 = (bf16[16,112,256]{2,1,0:T(8,128)(2,1)S(1)}, bf16[16,112,256]{2,1,0:T(8,128)(2,1)S(1)}, u32[]{:S(2)}, u32[]{:S(2)}) collective-permute-start(bf16[16,112,256]{2,1,0:T(8,128)(2,1)S(1)} %get-tuple-element.39), channel_id=1, source_target_pairs={{0,1},{1,0},{2,3},{3,2},{4,5},{5,4},{6,7},{7,6},{8,9},{9,8},{10,11... | collective-permute-start | bytes 2752520 | tf_op jit(solution)/shard_map/ppermute | solution.py:374
  70.8 25.8 %collective-permute-start.3 = (bf16[8,112,384]{2,1,0:T(8,128)(2,1)}, bf16[8,112,384]{2,1,0:T(8,128)(2,1)}, u32[]{:S(2)}, u32[]{:S(2)}) collective-permute-start(bf16[8,112,384]{2,1,0:T(8,128)(2,1)} %get-tuple-element.65), channel_id=1, source_target_pairs={{0,4},{1,5},{2,6},{3,7},{4,0},{5,1},{6,2},{7,3},{8,12},{9,13},{10,... | collective-permute-start | bytes 2064392 | tf_op jit(solution)/shard_map/ppermute | solution.py:374
  73.5 23.1 %collective-permute-start.1 = (bf16[8,112,384]{2,1,0:T(8,128)(2,1)}, bf16[8,112,384]{2,1,0:T(8,128)(2,1)}, u32[]{:S(2)}, u32[]{:S(2)}) collective-permute-start(bf16[8,112,384]{2,1,0:T(8,128)(2,1)} %get-tuple-element.66), channel_id=1, source_target_pairs={{0,2},{1,3},{2,0},{3,1},{4,6},{5,7},{6,4},{7,5},{8,10},{9,11},{10,... | collective-permute-start | bytes 2064392 | tf_op jit(solution)/shard_map/ppermute | solution.py:374
  76.0 20.6 %collective-permute-start.5 = (bf16[8,112,256]{2,1,0:T(8,128)(2,1)}, bf16[8,112,256]{2,1,0:T(8,128)(2,1)S(1)}, u32[]{:S(2)}, u32[]{:S(2)}) collective-permute-start(bf16[8,112,256]{2,1,0:T(8,128)(2,1)} %get-tuple-element.69), channel_id=1, source_target_pairs={{0,8},{1,9},{2,10},{3,11},{4,12},{5,13},{6,14},{7,15},{8,0},{9,1},... | collective-permute-start | bytes 1376264 | tf_op jit(solution)/shard_map/ppermute | solution.py:374
  76.0 47.5 %all-to-all-start.1 = ((bf16[32,64,256]{2,1,0:T(8,128)(2,1)}), bf16[32,64,256]{2,1,0:T(8,128)(2,1)S(1)}, u32[]{:S(2)}, u32[]{:S(2)}) async-start(bf16[32,64,256]{2,1,0:T(8,128)(2,1)} %bitcast.38), calls=%async_computation.1 | async-start | bytes 2097152 | tf_op jit(solution)/shard_map/all_to_all | solution.py:480
  97.9 14.6 %collective-permute-start.7 = (bf16[4,112,384]{2,1,0:T(8,128)(2,1)S(1)}, bf16[4,112,384]{2,1,0:T(8,128)(2,1)S(1)}, u32[]{:S(2)}, u32[]{:S(2)}) collective-permute-start(bf16[4,112,384]{2,1,0:T(8,128)(2,1)S(1)} %get-tuple-element.71), channel_id=1, source_target_pairs={{0,8},{1,9},{2,10},{3,11},{4,12},{5,13},{6,14},{7,15},{8,0},{9,1},... | collective-permute-start | bytes 1032200 | tf_op jit(solution)/shard_map/ppermute | solution.py:374
  99.4 13.0 %collective-permute-start.6 = (bf16[4,112,384]{2,1,0:T(8,128)(2,1)S(1)}, bf16[4,112,384]{2,1,0:T(8,128)(2,1)S(1)}, u32[]{:S(2)}, u32[]{:S(2)}) collective-permute-start(bf16[4,112,384]{2,1,0:T(8,128)(2,1)S(1)} %get-tuple-element.72), channel_id=1, source_target_pairs={{0,4},{1,5},{2,6},{3,7},{4,0},{5,1},{6,2},{7,3},{8,12},{9,13},{10,... | collective-permute-start | bytes 1032200 | tf_op jit(solution)/shard_map/ppermute | solution.py:374
  100.0 7.1 %collective-permute-start.8 = (bf16[4,112,256]{2,1,0:T(8,128)(2,1)S(1)}, bf16[4,112,256]{2,1,0:T(8,128)(2,1)S(1)}, u32[]{:S(2)}, u32[]{:S(2)}) collective-permute-start(bf16[4,112,256]{2,1,0:T(8,128)(2,1)S(1)} %get-tuple-element.75), channel_id=1, source_target_pairs={{0,2},{1,3},{2,0},{3,1},{4,6},{5,7},{6,4},{7,5},{8,10},{9,11},{10,... | collective-permute-start | bytes 688136 | tf_op jit(solution)/shard_map/ppermute | solution.py:374
  112.5 6.3 %collective-permute-start.10 = (bf16[2,112,384]{2,1,0:T(8,128)(2,1)S(1)}, bf16[2,112,384]{2,1,0:T(8,128)(2,1)S(1)}, u32[]{:S(2)}, u32[]{:S(2)}) collective-permute-start(bf16[2,112,384]{2,1,0:T(8,128)(2,1)S(1)} %get-tuple-element.77), channel_id=1, source_target_pairs={{0,2},{1,3},{2,0},{3,1},{4,6},{5,7},{6,4},{7,5},{8,10},{9,11},{10,... | collective-permute-start | bytes 516104 | tf_op jit(solution)/shard_map/ppermute | solution.py:374
  113.2 5.6 %collective-permute-start.9 = (bf16[2,112,384]{2,1,0:T(8,128)(2,1)S(1)}, bf16[2,112,384]{2,1,0:T(8,128)(2,1)S(1)}, u32[]{:S(2)}, u32[]{:S(2)}) collective-permute-start(bf16[2,112,384]{2,1,0:T(8,128)(2,1)S(1)} %get-tuple-element.78), channel_id=1, source_target_pairs={{0,8},{1,9},{2,10},{3,11},{4,12},{5,13},{6,14},{7,15},{8,0},{9,1},... | collective-permute-start | bytes 516104 | tf_op jit(solution)/shard_map/ppermute | solution.py:374
  113.9 4.9 %collective-permute-start.11 = (bf16[2,112,256]{2,1,0:T(8,128)(2,1)S(1)}, bf16[2,112,256]{2,1,0:T(8,128)(2,1)S(1)}, u32[]{:S(2)}, u32[]{:S(2)}) collective-permute-start(bf16[2,112,256]{2,1,0:T(8,128)(2,1)S(1)} %get-tuple-element.85), channel_id=1, source_target_pairs={{0,4},{1,5},{2,6},{3,7},{4,0},{5,1},{6,2},{7,3},{8,12},{9,13},{10,... | collective-permute-start | bytes 344072 | tf_op jit(solution)/shard_map/ppermute | solution.py:374
  118.8 10.9 %collective-permute-start.13 = (bf16[1,112,384]{2,1,0:T(8,128)(2,1)S(1)}, bf16[1,112,384]{2,1,0:T(8,128)(2,1)S(1)}, u32[]{:S(2)}, u32[]{:S(2)}) collective-permute-start(bf16[1,112,384]{2,1,0:T(8,128)(2,1)S(1)} %add_convert_fusion.21), channel_id=1, source_target_pairs={{0,16},{1,17},{2,18},{3,19},{4,20},{5,21},{6,22},{7,23},{8,24},{9,... | collective-permute-start | bytes 258056 | tf_op jit(solution)/shard_map/ppermute | solution.py:374
  120.4 9.3 %collective-permute-start.12 = (bf16[1,112,384]{2,1,0:T(8,128)(2,1)S(1)}, bf16[1,112,384]{2,1,0:T(8,128)(2,1)S(1)}, u32[]{:S(2)}, u32[]{:S(2)}) collective-permute-start(bf16[1,112,384]{2,1,0:T(8,128)(2,1)S(1)} %add_convert_fusion.22), channel_id=1, source_target_pairs={{0,16},{1,17},{2,18},{3,19},{4,20},{5,21},{6,22},{7,23},{8,24},{9,... | collective-permute-start | bytes 258056 | tf_op jit(solution)/shard_map/ppermute | solution.py:374
  121.9 7.8 %collective-permute-start.14 = (bf16[1,112,256]{2,1,0:T(8,128)(2,1)S(1)}, bf16[1,112,256]{2,1,0:T(8,128)(2,1)S(1)}, u32[]{:S(2)}, u32[]{:S(2)}) collective-permute-start(bf16[1,112,256]{2,1,0:T(8,128)(2,1)S(1)} %add_convert_fusion.26), channel_id=1, source_target_pairs={{0,16},{1,17},{2,18},{3,19},{4,20},{5,21},{6,22},{7,23},{8,24},{9,... | collective-permute-start | bytes 172040 | tf_op jit(solution)/shard_map/ppermute | solution.py:374
  (2 other events, 2.0 us)

commit v4 on v3

--- a/solution.py
+++ b/solution.py
@@ -377,10 +377,41 @@
         if k:
             got = lax.optimization_barrier(got)
         if k == stages - 1:
-            return [add_pair(a, b)[0] for a, b in zip(los, got)]
+            return los, list(got)
         n = los[0].shape[0] // 2
         his = [add_pair(a[n:], b[n:]) for a, b in zip(los, got)]
         los = [add_pair(a[:n], b[:n]) for a, b in zip(los, got)]
+
+
+def finish(mine, got, rank, chunk):
+    colors = len(mine)
+
+    def kernel(*refs):
+        in_ref, out_ref, bias_ref = refs[2 * colors :]
+        sums = [a[0].astype(F32) + b[0].astype(F32) for a, b in zip(refs[:colors], refs[colors : 2 * colors])]
+        targets = ((out_ref, 1), (in_ref, 1), (out_ref, 0), (in_ref, 0))
+        at = 0
+        for x in sums:
+            done = 0
+            while done < x.shape[1]:
+                target, layer = targets[at // rank]
+                size = min(x.shape[1] - done, rank - at % rank)
+                target[:, layer, at % rank : at % rank + size] = x[:chunk, done : done + size]
+                done += size
+                at += size
+        bias_ref[0:1, :] = sums[1][chunk : chunk + 1, :chunk]
+        bias_ref[1:2, :] = sums[0][chunk : chunk + 1, :chunk]
+
+    vmem = pl.BlockSpec(memory_space=pltpu.VMEM)
+    wide = jax.ShapeDtypeStruct((chunk, 2, rank), F32)
+    return pl.pallas_call(
+        kernel,
+        in_specs=[vmem] * (2 * colors),
+        out_specs=[vmem] * 3,
+        out_shape=[wide, wide, jax.ShapeDtypeStruct((2, chunk), F32)],
+        compiler_params=pltpu.CompilerParams(vmem_limit_bytes=16 << 20),
+        name="finish",
+    )(*mine, *got)
 
 
 def run(
@@ -486,14 +517,11 @@
         [[(0, 1, 0, rank), (1, 2, 0, cut)], [(1, 2, cut, rank), (2, 0, 0, rank)], [(3, 3, 0, rank)]],
         [0, 2, None], orders, *fixed,
     )
-    sums = reduce_pieces(los, his, orders, devices)
+    mine, got = reduce_pieces(los, his, orders, devices)
+    grad_in, grad_out, grad_bias = finish(mine, got, rank, chunk)
+    grad_in = jnp.transpose(grad_in, (1, 0, 2))
+    grad_out = jnp.transpose(grad_out, (1, 2, 0))
     pooled_grad = unpack(back)
-    bias1, bias0 = sums[0][chunk, :chunk], sums[1][chunk, :chunk]
-    flat = jnp.concatenate([x[:chunk] for x in sums], 1).astype(F32)
-    out1, in1, out0, in0 = [flat[:, i * rank : (i + 1) * rank] for i in range(4)]
-    grad_in = jnp.transpose(jnp.stack([in0, in1], 1), (1, 0, 2))
-    grad_out = jnp.transpose(jnp.stack([out0, out1], 1), (1, 2, 0))
-    grad_bias = jnp.stack([bias0, bias1]).astype(F32)
     return (pooled_grad, grad_in, grad_out, grad_bias)
 
 

time: 133 us -> 131 us (0.985)
  local copies, waits for them, and re-layouts: 19.5 us -> 17.7 us
    unnamed x25 -> x23, local copies, waits for them, and re-layouts: 16 us -> 14.2 us
    convert_element_type x13 -> x12, other arithmetic: 6.37 us -> 6.39 us  [add_pair(): return (a.astype(F32) + b.astype(F32)).astype(BF)]
where the time goes in v4:
time: 131 us
  waiting for transfers between devices  46.7 us (36%)
  Pallas kernels  34.5 us (26%)
  starting transfers between devices  23.3 us (18%)
  local copies, waits for them, and re-layouts  17.7 us (14%)
  other arithmetic  7.64 us (6%)
    ppermute x15, waiting for transfers between devices, reduce_pieces(): lax.ppermute(h, AXES, [(i, i ^ o[k]) for i in range(devices)])  36.1 us
    pallas_call x1, Pallas kernels, run(): pl.pallas_call(make_step(tables, devices, blocks_here), in_specs=[smem] +...  16.4 us
    unnamed x23, local copies, waits for them, and re-layouts  14.2 us
    ppermute x15, starting transfers between devices, reduce_pieces(): lax.ppermute(h, AXES, [(i, i ^ o[k]) for i in range(devices)])  13 us
    all_to_all x1, waiting for transfers between devices, run(): lax.all_to_all(pack(pooled, sample_weight, devices), AXES, 0, 0, tiled=True)  10.7 us
    pallas_call x1, Pallas kernels, weight_grads(): pl.pallas_call(make_grads(pieces, biases, orders, cols, devices, chunk, c...  10.1 us
    all_to_all x1, starting transfers between devices, run(): lax.all_to_all(pack(pooled, sample_weight, devices), AXES, 0, 0, tiled=True)  7.44 us
    convert_element_type x12, other arithmetic, add_pair(): return (a.astype(F32) + b.astype(F32)).astype(BF)  6.39 us
  transfers between devices with their start and end apart: 17, of which 7 were waited for; matrix products, arithmetic and copies ran while one was open for 18% of the time, Pallas kernels for 3%

profile of v4, /device:TPU:0, one launch (start us, length us, event | category | flops | bytes accessed | tf_op | source)
XLA Modules:
  0.0 130.7 jit_solution(8544066382651067885)
XLA Ops:
  0.6 3.2 %pack.1 = bf16[32,136,128]{2,1,0:T(8,128)(2,1)} custom-call(f32[2,128]{1,0:T(2,128)} %bitcast.22, bf16[16,4,8192]{2,1,0:T(4,128)(2,1)} %x_ref.1), custom_call_target="tpu_custom_call" | custom-call | tf_op jit(solution)/shard_map/pack/pallas_call | solution.py:85
  3.8 7.4 %all-to-all-start = ((bf16[32,136,128]{2,1,0:T(8,128)(2,1)}), bf16[32,136,128]{2,1,0:T(8,128)(2,1)}, u32[]{:S(2)}, u32[]{:S(2)}) async-start(bf16[32,136,128]{2,1,0:T(8,128)(2,1)} %pack.1), calls=%async_computation | async-start | bytes 2228224 | tf_op jit(solution)/shard_map/all_to_all | solution.py:456
  12.8 2.6 %copy.34.col_hbm = f32[3456,3]{1,0:T(8,128)} copy(f32[3456,3]{0,1:T(4,128)} %pad_maximum_fusion) | data formatting | bytes 82944 | tf_op jit(solution)/shard_map/stack | solution.py:458
  15.4 3.7 %copy.32 = bf16[2,3456,256]{1,2,0:T(8,128)(2,1)} copy(bf16[2,3456,256]{2,1,0:T(8,128)(2,1)S(1)} %copy-done.1) | data formatting | bytes 7077888 | tf_op args[8]
  19.1 5.8 %copy.33 = bf16[2,256,3456]{1,2,0:T(8,128)(2,1)} copy(bf16[2,256,3456]{2,1,0:T(8,128)(2,1)} %co_hbm.1) | data formatting | bytes 7077888 | tf_op args[9]
  28.2 10.7 %all-to-all-done.x_ref = bf16[32,136,128]{2,1,0:T(8,128)(2,1)} async-done(((bf16[32,136,128]{2,1,0:T(8,128)(2,1)}), bf16[32,136,128]{2,1,0:T(8,128)(2,1)}, u32[]{:S(2)}, u32[]{:S(2)}) %all-to-all-start) | async-done | bytes 1114144 | tf_op jit(solution)/shard_map/all_to_all | solution.py:456
  38.8 16.4 %step.1 = (bf16[128,16,256]{2,1,0:T(8,128)(2,1)}, bf16[3456,256]{1,0:T(8,128)(2,1)}, bf16[3456,256]{1,0:T(8,128)(2,1)}, bf16[3456,256]{1,0:T(8,128)(2,1)}, bf16[...) custom-call(s32[128]{0:T(128)} %slot_ref.1, bf16[32,136,128]{2,1,0:T(8,128)(2,1)} %all-to-all-done.x_ref, ...), custom_call_target="tpu_custom_call" | custom-call | flops 3623878656 | bytes 20971520 | tf_op jit(solution)/shard_map/step/pallas_call | solution.py:465
  56.3 10.1 %shard_map.147 = (bf16[16,112,384]{2,1,0:T(8,128)(2,1)S(1)}, bf16[16,112,384]{2,1,0:T(8,128)(2,1)S(1)}, bf16[16,112,256]{2,1,0:T(8,128)(2,1)S(1)}, bf16[16,112,3...) custom-call(s32[1]{0:T(128)} %bitcast.11.me_ref, ...), custom_call_target="tpu_custom_call" | custom-call | flops 1811939328 | bytes 14155776 | tf_op jit(solution)/shard_map/pallas_call | solution.py:350
  67.1 2.5 %collective-permute-done.2 = bf16[16,112,384]{2,1,0:T(8,128)(2,1)S(1)} collective-permute-done((bf16[16,112,384]{2,1,0:T(8,128)(2,1)S(1)}, bf16[16,112,384]{2,1,0:T(8,128)(2,1)S(1)}, u32[]{:S(2)}, u32[]{:S(2)}) %collective-permute-start.2) | collective-permute-done | bytes 1376288 | tf_op jit(solution)/shard_map/ppermute | solution.py:374
  70.9 1.5 %collective-permute-start.3 = (bf16[8,112,384]{2,1,0:T(8,128)(2,1)}, bf16[8,112,384]{2,1,0:T(8,128)(2,1)}, u32[]{:S(2)}, u32[]{:S(2)}) collective-permute-start(bf16[8,112,384]{2,1,0:T(8,128)(2,1)} %get-tuple-element.59), channel_id=1, source_target_pairs={{0,4},{1,5},{2,6},{3,7},{4,0},{5,1},{6,2},{7,3},{8,12},{9,13},{10,... | collective-permute-start | bytes 2064392 | tf_op jit(solution)/shard_map/ppermute | solution.py:374
  73.5 1.5 %collective-permute-start.1 = (bf16[8,112,384]{2,1,0:T(8,128)(2,1)}, bf16[8,112,384]{2,1,0:T(8,128)(2,1)}, u32[]{:S(2)}, u32[]{:S(2)}) collective-permute-start(bf16[8,112,384]{2,1,0:T(8,128)(2,1)} %get-tuple-element.60), channel_id=1, source_target_pairs={{0,2},{1,3},{2,0},{3,1},{4,6},{5,7},{6,4},{7,5},{8,10},{9,11},{10,... | collective-permute-start | bytes 2064392 | tf_op jit(solution)/shard_map/ppermute | solution.py:374
  76.0 2.9 %all-to-all-start.1 = ((bf16[32,64,256]{2,1,0:T(8,128)(2,1)}), bf16[32,64,256]{2,1,0:T(8,128)(2,1)S(1)}, u32[]{:S(2)}, u32[]{:S(2)}) async-start(bf16[32,64,256]{2,1,0:T(8,128)(2,1)} %bitcast.20), calls=%async_computation.1 | async-start | bytes 2097152 | tf_op jit(solution)/shard_map/all_to_all | solution.py:511
  78.9 17.7 %collective-permute-done.5 = bf16[8,112,256]{2,1,0:T(8,128)(2,1)S(1)} collective-permute-done((bf16[8,112,256]{2,1,0:T(8,128)(2,1)}, bf16[8,112,256]{2,1,0:T(8,128)(2,1)S(1)}, u32[]{:S(2)}, u32[]{:S(2)}) %collective-permute-start.5) | collective-permute-done | bytes 458784 | tf_op jit(solution)/shard_map/ppermute | solution.py:374
  96.7 1.3 add_convert_fusion.6
  98.2 1.3 add_convert_fusion.8
  100.1 1.7 %collective-permute-start.8 = (bf16[4,112,256]{2,1,0:T(8,128)(2,1)S(1)}, bf16[4,112,256]{2,1,0:T(8,128)(2,1)S(1)}, u32[]{:S(2)}, u32[]{:S(2)}) collective-permute-start(bf16[4,112,256]{2,1,0:T(8,128)(2,1)S(1)} %get-tuple-element.69), channel_id=1, source_target_pairs={{0,2},{1,3},{2,0},{3,1},{4,6},{5,7},{6,4},{7,5},{8,10},{9,11},{10,... | collective-permute-start | bytes 688136 | tf_op jit(solution)/shard_map/ppermute | solution.py:374
  101.8 5.4 %collective-permute-done.8 = bf16[4,112,256]{2,1,0:T(8,128)(2,1)S(1)} collective-permute-done((bf16[4,112,256]{2,1,0:T(8,128)(2,1)S(1)}, bf16[4,112,256]{2,1,0:T(8,128)(2,1)S(1)}, u32[]{:S(2)}, u32[]{:S(2)}) %collective-permute-start.8) | collective-permute-done | bytes 229408 | tf_op jit(solution)/shard_map/ppermute | solution.py:374
  107.2 5.3 %collective-permute-done.7 = bf16[4,112,384]{2,1,0:T(8,128)(2,1)S(1)} collective-permute-done((bf16[4,112,384]{2,1,0:T(8,128)(2,1)S(1)}, bf16[4,112,384]{2,1,0:T(8,128)(2,1)S(1)}, u32[]{:S(2)}, u32[]{:S(2)}) %collective-permute-start.7) | collective-permute-done | bytes 344096 | tf_op jit(solution)/shard_map/ppermute | solution.py:374
  115.0 3.8 %collective-permute-done.11 = bf16[2,112,256]{2,1,0:T(8,128)(2,1)S(1)} collective-permute-done((bf16[2,112,256]{2,1,0:T(8,128)(2,1)S(1)}, bf16[2,112,256]{2,1,0:T(8,128)(2,1)S(1)}, u32[]{:S(2)}, u32[]{:S(2)}) %collective-permute-start.11) | collective-permute-done | bytes 114720 | tf_op jit(solution)/shard_map/ppermute | solution.py:374
  118.9 1.5 %collective-permute-start.13 = (bf16[1,112,384]{2,1,0:T(8,128)(2,1)S(1)}, bf16[1,112,384]{2,1,0:T(8,128)(2,1)S(1)}, u32[]{:S(2)}, u32[]{:S(2)}) collective-permute-start(bf16[1,112,384]{2,1,0:T(8,128)(2,1)S(1)} %get-tuple-element.76), channel_id=1, source_target_pairs={{0,16},{1,17},{2,18},{3,19},{4,20},{5,21},{6,22},{7,23},{8,24},{9,... | collective-permute-start | bytes 258056 | tf_op jit(solution)/shard_map/ppermute | solution.py:374
  120.5 1.5 %collective-permute-start.12 = (bf16[1,112,384]{2,1,0:T(8,128)(2,1)S(1)}, bf16[1,112,384]{2,1,0:T(8,128)(2,1)S(1)}, u32[]{:S(2)}, u32[]{:S(2)}) collective-permute-start(bf16[1,112,384]{2,1,0:T(8,128)(2,1)S(1)} %get-tuple-element.78), channel_id=1, source_target_pairs={{0,16},{1,17},{2,18},{3,19},{4,20},{5,21},{6,22},{7,23},{8,24},{9,... | collective-permute-start | bytes 258056 | tf_op jit(solution)/shard_map/ppermute | solution.py:374
  122.0 1.5 %collective-permute-start.14 = (bf16[1,112,256]{2,1,0:T(8,128)(2,1)S(1)}, bf16[1,112,256]{2,1,0:T(8,128)(2,1)S(1)}, u32[]{:S(2)}, u32[]{:S(2)}) collective-permute-start(bf16[1,112,256]{2,1,0:T(8,128)(2,1)S(1)} %get-tuple-element.80), channel_id=1, source_target_pairs={{0,16},{1,17},{2,18},{3,19},{4,20},{5,21},{6,22},{7,23},{8,24},{9,... | collective-permute-start | bytes 172040 | tf_op jit(solution)/shard_map/ppermute | solution.py:374
  124.6 4.0 %unpack.1 = f32[16,4,8192]{2,1,0:T(4,128)} custom-call(bf16[32,64,256]{2,1,0:T(8,128)(2,1)} %copy-done.2), custom_call_target="tpu_custom_call" | custom-call | tf_op jit(solution)/shard_map/unpack/pallas_call | solution.py:116
  128.5 1.2 collective-permute-done.14.refs_5_
  (56 shorter events, 15.4 us)
Async XLA Ops:
  0.6 10.6 %copy-start.6 = (f32[3456]{0:T(1024)S(1)}, f32[3456]{0:T(1024)}, u32[]{:S(2)}) copy-start(f32[3456]{0:T(1024)} %param.23) | copy-start | bytes 41476
  3.8 11.6 %copy-start.1 = (bf16[2,3456,256]{2,1,0:T(8,128)(2,1)S(1)}, bf16[2,3456,256]{2,1,0:T(8,128)(2,1)}, u32[]{:S(2)}) copy-start(bf16[2,3456,256]{2,1,0:T(8,128)(2,1)} %ci_hbm.1) | copy-start | bytes 10616836
  3.8 35.0 %all-to-all-start = ((bf16[32,136,128]{2,1,0:T(8,128)(2,1)}), bf16[32,136,128]{2,1,0:T(8,128)(2,1)}, u32[]{:S(2)}, u32[]{:S(2)}) async-start(bf16[32,136,128]{2,1,0:T(8,128)(2,1)} %pack.1), calls=%async_computation | async-start | bytes 2228224 | tf_op jit(solution)/shard_map/all_to_all | solution.py:456
  19.1 5.8 %copy-start.5 = (bf16[16,16,128]{2,1,0:T(8,128)(2,1)S(1)}, bf16[16,16,128]{2,1,0:T(8,128)(2,1)}, u32[]{:S(2)}) copy-start(bf16[16,16,128]{2,1,0:T(8,128)(2,1)} %p2.1) | copy-start | bytes 196612
  19.1 6.8 %copy-start.3 = (bf16[6,256,128]{2,1,0:T(8,128)(2,1)S(1)}, bf16[6,256,128]{2,1,0:T(8,128)(2,1)}, u32[]{:S(2)}) copy-start(bf16[6,256,128]{2,1,0:T(8,128)(2,1)} %p0.1) | copy-start | bytes 1179652
  24.9 2.0 %copy-start.4 = (bf16[4,64,128]{2,1,0:T(8,128)(2,1)S(1)}, bf16[4,64,128]{2,1,0:T(8,128)(2,1)}, u32[]{:S(2)}) copy-start(bf16[4,64,128]{2,1,0:T(8,128)(2,1)} %p1.1) | copy-start | bytes 196612
  24.9 2.7 %copy-start.8 = (s32[256]{0:T(256)S(1)}, s32[256]{0:T(256)}, u32[]{:S(2)}) copy-start(s32[256]{0:T(256)} %param.15) | copy-start | bytes 3076
  24.9 2.7 %copy-start.7 = (f32[256]{0:T(256)S(1)}, f32[256]{0:T(256)}, u32[]{:S(2)}) copy-start(f32[256]{0:T(256)} %param.16) | copy-start | bytes 3076
  66.5 3.2 %collective-permute-start.2 = (bf16[16,112,384]{2,1,0:T(8,128)(2,1)S(1)}, bf16[16,112,384]{2,1,0:T(8,128)(2,1)S(1)}, u32[]{:S(2)}, u32[]{:S(2)}) collective-permute-start(bf16[16,112,384]{2,1,0:T(8,128)(2,1)S(1)} %get-tuple-element.40), channel_id=1, source_target_pairs={{0,1},{1,0},{2,3},{3,2},{4,5},{5,4},{6,7},{7,6},{8,9},{9,8},{10,11... | collective-permute-start | bytes 4128776 | tf_op jit(solution)/shard_map/ppermute | solution.py:374
  66.5 5.8 %collective-permute-start = (bf16[16,112,384]{2,1,0:T(8,128)(2,1)S(1)}, bf16[16,112,384]{2,1,0:T(8,128)(2,1)S(1)}, u32[]{:S(2)}, u32[]{:S(2)}) collective-permute-start(bf16[16,112,384]{2,1,0:T(8,128)(2,1)S(1)} %get-tuple-element.38), channel_id=1, source_target_pairs={{0,1},{1,0},{2,3},{3,2},{4,5},{5,4},{6,7},{7,6},{8,9},{9,8},{10,11... | collective-permute-start | bytes 4128776 | tf_op jit(solution)/shard_map/ppermute | solution.py:374
  67.0 8.0 %collective-permute-start.4 = (bf16[16,112,256]{2,1,0:T(8,128)(2,1)S(1)}, bf16[16,112,256]{2,1,0:T(8,128)(2,1)S(1)}, u32[]{:S(2)}, u32[]{:S(2)}) collective-permute-start(bf16[16,112,256]{2,1,0:T(8,128)(2,1)S(1)} %get-tuple-element.42), channel_id=1, source_target_pairs={{0,1},{1,0},{2,3},{3,2},{4,5},{5,4},{6,7},{7,6},{8,9},{9,8},{10,11... | collective-permute-start | bytes 2752520 | tf_op jit(solution)/shard_map/ppermute | solution.py:374
  70.9 25.8 %collective-permute-start.3 = (bf16[8,112,384]{2,1,0:T(8,128)(2,1)}, bf16[8,112,384]{2,1,0:T(8,128)(2,1)}, u32[]{:S(2)}, u32[]{:S(2)}) collective-permute-start(bf16[8,112,384]{2,1,0:T(8,128)(2,1)} %get-tuple-element.59), channel_id=1, source_target_pairs={{0,4},{1,5},{2,6},{3,7},{4,0},{5,1},{6,2},{7,3},{8,12},{9,13},{10,... | collective-permute-start | bytes 2064392 | tf_op jit(solution)/shard_map/ppermute | solution.py:374
  73.5 23.1 %collective-permute-start.1 = (bf16[8,112,384]{2,1,0:T(8,128)(2,1)}, bf16[8,112,384]{2,1,0:T(8,128)(2,1)}, u32[]{:S(2)}, u32[]{:S(2)}) collective-permute-start(bf16[8,112,384]{2,1,0:T(8,128)(2,1)} %get-tuple-element.60), channel_id=1, source_target_pairs={{0,2},{1,3},{2,0},{3,1},{4,6},{5,7},{6,4},{7,5},{8,10},{9,11},{10,... | collective-permute-start | bytes 2064392 | tf_op jit(solution)/shard_map/ppermute | solution.py:374
  76.0 20.6 %collective-permute-start.5 = (bf16[8,112,256]{2,1,0:T(8,128)(2,1)}, bf16[8,112,256]{2,1,0:T(8,128)(2,1)S(1)}, u32[]{:S(2)}, u32[]{:S(2)}) collective-permute-start(bf16[8,112,256]{2,1,0:T(8,128)(2,1)} %get-tuple-element.63), channel_id=1, source_target_pairs={{0,8},{1,9},{2,10},{3,11},{4,12},{5,13},{6,14},{7,15},{8,0},{9,1},... | collective-permute-start | bytes 1376264 | tf_op jit(solution)/shard_map/ppermute | solution.py:374
  76.0 47.5 %all-to-all-start.1 = ((bf16[32,64,256]{2,1,0:T(8,128)(2,1)}), bf16[32,64,256]{2,1,0:T(8,128)(2,1)S(1)}, u32[]{:S(2)}, u32[]{:S(2)}) async-start(bf16[32,64,256]{2,1,0:T(8,128)(2,1)} %bitcast.20), calls=%async_computation.1 | async-start | bytes 2097152 | tf_op jit(solution)/shard_map/all_to_all | solution.py:511
  97.9 14.6 %collective-permute-start.7 = (bf16[4,112,384]{2,1,0:T(8,128)(2,1)S(1)}, bf16[4,112,384]{2,1,0:T(8,128)(2,1)S(1)}, u32[]{:S(2)}, u32[]{:S(2)}) collective-permute-start(bf16[4,112,384]{2,1,0:T(8,128)(2,1)S(1)} %get-tuple-element.65), channel_id=1, source_target_pairs={{0,8},{1,9},{2,10},{3,11},{4,12},{5,13},{6,14},{7,15},{8,0},{9,1},... | collective-permute-start | bytes 1032200 | tf_op jit(solution)/shard_map/ppermute | solution.py:374
  99.5 13.0 %collective-permute-start.6 = (bf16[4,112,384]{2,1,0:T(8,128)(2,1)S(1)}, bf16[4,112,384]{2,1,0:T(8,128)(2,1)S(1)}, u32[]{:S(2)}, u32[]{:S(2)}) collective-permute-start(bf16[4,112,384]{2,1,0:T(8,128)(2,1)S(1)} %get-tuple-element.66), channel_id=1, source_target_pairs={{0,4},{1,5},{2,6},{3,7},{4,0},{5,1},{6,2},{7,3},{8,12},{9,13},{10,... | collective-permute-start | bytes 1032200 | tf_op jit(solution)/shard_map/ppermute | solution.py:374
  100.1 7.1 %collective-permute-start.8 = (bf16[4,112,256]{2,1,0:T(8,128)(2,1)S(1)}, bf16[4,112,256]{2,1,0:T(8,128)(2,1)S(1)}, u32[]{:S(2)}, u32[]{:S(2)}) collective-permute-start(bf16[4,112,256]{2,1,0:T(8,128)(2,1)S(1)} %get-tuple-element.69), channel_id=1, source_target_pairs={{0,2},{1,3},{2,0},{3,1},{4,6},{5,7},{6,4},{7,5},{8,10},{9,11},{10,... | collective-permute-start | bytes 688136 | tf_op jit(solution)/shard_map/ppermute | solution.py:374
  112.6 6.3 %collective-permute-start.10 = (bf16[2,112,384]{2,1,0:T(8,128)(2,1)S(1)}, bf16[2,112,384]{2,1,0:T(8,128)(2,1)S(1)}, u32[]{:S(2)}, u32[]{:S(2)}) collective-permute-start(bf16[2,112,384]{2,1,0:T(8,128)(2,1)S(1)} %get-tuple-element.71), channel_id=1, source_target_pairs={{0,2},{1,3},{2,0},{3,1},{4,6},{5,7},{6,4},{7,5},{8,10},{9,11},{10,... | collective-permute-start | bytes 516104 | tf_op jit(solution)/shard_map/ppermute | solution.py:374
  113.3 5.6 %collective-permute-start.9 = (bf16[2,112,384]{2,1,0:T(8,128)(2,1)S(1)}, bf16[2,112,384]{2,1,0:T(8,128)(2,1)S(1)}, u32[]{:S(2)}, u32[]{:S(2)}) collective-permute-start(bf16[2,112,384]{2,1,0:T(8,128)(2,1)S(1)} %get-tuple-element.72), channel_id=1, source_target_pairs={{0,8},{1,9},{2,10},{3,11},{4,12},{5,13},{6,14},{7,15},{8,0},{9,1},... | collective-permute-start | bytes 516104 | tf_op jit(solution)/shard_map/ppermute | solution.py:374
  114.0 4.9 %collective-permute-start.11 = (bf16[2,112,256]{2,1,0:T(8,128)(2,1)S(1)}, bf16[2,112,256]{2,1,0:T(8,128)(2,1)S(1)}, u32[]{:S(2)}, u32[]{:S(2)}) collective-permute-start(bf16[2,112,256]{2,1,0:T(8,128)(2,1)S(1)} %get-tuple-element.75), channel_id=1, source_target_pairs={{0,4},{1,5},{2,6},{3,7},{4,0},{5,1},{6,2},{7,3},{8,12},{9,13},{10,... | collective-permute-start | bytes 344072 | tf_op jit(solution)/shard_map/ppermute | solution.py:374
  118.9 10.9 %collective-permute-start.13 = (bf16[1,112,384]{2,1,0:T(8,128)(2,1)S(1)}, bf16[1,112,384]{2,1,0:T(8,128)(2,1)S(1)}, u32[]{:S(2)}, u32[]{:S(2)}) collective-permute-start(bf16[1,112,384]{2,1,0:T(8,128)(2,1)S(1)} %get-tuple-element.76), channel_id=1, source_target_pairs={{0,16},{1,17},{2,18},{3,19},{4,20},{5,21},{6,22},{7,23},{8,24},{9,... | collective-permute-start | bytes 258056 | tf_op jit(solution)/shard_map/ppermute | solution.py:374
  120.5 9.3 %collective-permute-start.12 = (bf16[1,112,384]{2,1,0:T(8,128)(2,1)S(1)}, bf16[1,112,384]{2,1,0:T(8,128)(2,1)S(1)}, u32[]{:S(2)}, u32[]{:S(2)}) collective-permute-start(bf16[1,112,384]{2,1,0:T(8,128)(2,1)S(1)} %get-tuple-element.78), channel_id=1, source_target_pairs={{0,16},{1,17},{2,18},{3,19},{4,20},{5,21},{6,22},{7,23},{8,24},{9,... | collective-permute-start | bytes 258056 | tf_op jit(solution)/shard_map/ppermute | solution.py:374
  122.0 7.7 %collective-permute-start.14 = (bf16[1,112,256]{2,1,0:T(8,128)(2,1)S(1)}, bf16[1,112,256]{2,1,0:T(8,128)(2,1)S(1)}, u32[]{:S(2)}, u32[]{:S(2)}) collective-permute-start(bf16[1,112,256]{2,1,0:T(8,128)(2,1)S(1)} %get-tuple-element.80), channel_id=1, source_target_pairs={{0,16},{1,17},{2,18},{3,19},{4,20},{5,21},{6,22},{7,23},{8,24},{9,... | collective-permute-start | bytes 172040 | tf_op jit(solution)/shard_map/ppermute | solution.py:374
  (2 other events, 2.0 us)
